TPU v7x, 256 devices: a whole 4x4x8 slice. The times are simulated.
256 devices in a mesh: dp: 32 (over y, x, core), seq: 8 (over z).
Axes of the slice: x: 4, y: 4, z: 8, core: 2. Of those that a mesh axis runs over, the one named last changes fastest.
Arguments:
- query_rows: bfloat16 [32, 1024, 3072], P('dp', 'seq'), may hold values from -6 to 6
- key_rows: bfloat16 [32, 1024, 3072], P('dp', 'seq'), may hold values from -6 to 6
- value_rows: bfloat16 [32, 1024, 3072], P('dp', 'seq'), may hold values from -6 to 6
- out_grad: bfloat16 [32, 1024, 6144], P('dp', 'seq'), may hold values from -54 to 54
- clip_lengths: int32 [32, 4], P('dp'), may hold values from 1 to 512, 1024 in all within a row
- out_weight: bfloat16 [3072, 6144], P('seq'), may hold values from -0.109375 to 0.109375
- query_gain: float32 [128], replicated, may hold values from 0.1 to 1.9
- key_gain: float32 [128], replicated, may hold values from 0.1 to 1.9
Outputs:
- query_grad: bfloat16 [32, 1024, 3072], P('dp', 'seq')
- key_grad: bfloat16 [32, 1024, 3072], P('dp', 'seq')
- value_grad: bfloat16 [32, 1024, 3072], P('dp', 'seq')
- weight_grad: float32 [3072, 6144], P('seq', 'dp')
- querygain_grad: float32 [128], replicated
- keygain_grad: float32 [128], replicated
- grad_norm: float32 [], replicated
Inputs may be any that keep to these rules, and one draw needn't show every extreme that they name: `clip_lengths`: the token counts of each group's clips sum to 1024.
All inputs are finite; a program needn't handle non-finite values.
Results may differ from a plain program's by a relative error of at most 0.015.
Values may be sent and summed in bfloat16 or wider, within the bound.
A program may use at most 128 MiB of HBM per device.

v0:
```python
import jax
import jax.numpy as jnp
from jax import lax
from jax.sharding import Mesh
from jax.sharding import PartitionSpec as P

HEAD_DIM = 128
MAX_NORM = 768
DP = ("dp_0", "dp_1", "dp_2")
DP_SEQ = ("dp_0", "dp_1", "dp_2", "seq")


EPS = 1e-06


def one_axis_at_a_time(array, axes):
    for axis in axes:
        array = lax.psum(array, axis)
    return array


def segment_ids(lengths, total):
    ends = jnp.cumsum(lengths)
    places = jnp.arange(total, dtype=jnp.int32)
    return jnp.sum((places[:, None] >= ends[None, :]).astype(jnp.int32), axis=1)


def norm_rows(rows, gain):
    wide = rows.astype(jnp.float32)
    inverse = lax.rsqrt(jnp.mean(wide * wide, axis=-1, keepdims=True) + EPS)
    unit = wide * inverse
    return (unit, inverse, (unit * gain).astype(jnp.bfloat16))


def norm_back(unit, inverse, gain, d_norm):
    gain_part = jnp.sum(unit * d_norm, axis=(0, 1))
    d_unit = d_norm * gain
    d_rows = inverse * (d_unit - unit * jnp.mean(unit * d_unit, axis=-1, keepdims=True))
    return (d_rows.astype(jnp.bfloat16), gain_part)


def local(
    query_rows, key_rows, value_rows, out_grad, clip_lengths, out_weight, query_gain, key_gain
):
    query, keys, values = (
        lax.all_to_all(query_rows[0], "seq", split_axis=1, concat_axis=0, tiled=True),
        lax.all_to_all(key_rows[0], "seq", split_axis=1, concat_axis=0, tiled=True),
        lax.all_to_all(value_rows[0], "seq", split_axis=1, concat_axis=0, tiled=True),
    )
    total = query.shape[0]
    heads = query.shape[1] // HEAD_DIM
    width = heads * HEAD_DIM
    scale = HEAD_DIM ** (-0.5)
    block = min(512, total)
    blocks = total // block
    seg = segment_ids(clip_lengths[0], total)
    q_unit, q_inv, q_norm = norm_rows(query.reshape(total, heads, HEAD_DIM), query_gain)
    k_unit, k_inv, k_norm = norm_rows(keys.reshape(total, heads, HEAD_DIM), key_gain)
    values3 = values.reshape(total, heads, HEAD_DIM)

    def forward_block(index):
        start = index * block
        query_block = lax.dynamic_slice_in_dim(q_norm, start, block, 0)
        seg_block = lax.dynamic_slice_in_dim(seg, start, block, 0)
        scores = (
            jnp.einsum("qhd,khd->hqk", query_block, k_norm, preferred_element_type=jnp.float32)
            * scale
        )
        same = seg_block[:, None] == seg[None, :]
        expo = jnp.where(same[None], jnp.exp(scores), 0.0)
        probs = (expo / jnp.sum(expo, axis=-1, keepdims=True)).astype(jnp.bfloat16)
        attn_out = jnp.einsum("hqk,khd->qhd", probs, values3, preferred_element_type=jnp.float32)
        return (probs, attn_out.astype(jnp.bfloat16))

    probs_all, attn_blocks = lax.map(forward_block, jnp.arange(blocks, dtype=jnp.int32))
    attn_flat = attn_blocks.reshape(total, width)
    out_full = lax.all_gather(out_grad[0], "seq", axis=0, tiled=True)
    weight_part = jnp.dot(attn_flat.T, out_full, preferred_element_type=jnp.float32)
    d_attn = jnp.dot(out_full, out_weight.T, preferred_element_type=jnp.float32).astype(
        jnp.bfloat16
    )
    d_attn3 = d_attn.reshape(total, heads, HEAD_DIM)

    def backward_block(carry, items):
        d_key, d_value = carry
        probs, index = items
        start = index * block
        attn_grad = lax.dynamic_slice_in_dim(d_attn3, start, block, 0)
        query_block = lax.dynamic_slice_in_dim(q_norm, start, block, 0)
        d_probs = jnp.einsum("qhd,khd->hqk", attn_grad, values3, preferred_element_type=jnp.float32)
        probs32 = probs.astype(jnp.float32)
        row_sum = jnp.sum(probs32 * d_probs, axis=-1, keepdims=True)
        d_scores = (probs32 * (d_probs - row_sum) * scale).astype(jnp.bfloat16)
        d_value = d_value + jnp.einsum(
            "hqk,qhd->khd", probs, attn_grad, preferred_element_type=jnp.float32
        )
        d_key = d_key + jnp.einsum(
            "hqk,qhd->khd", d_scores, query_block, preferred_element_type=jnp.float32
        )
        d_query = jnp.einsum("hqk,khd->qhd", d_scores, k_norm, preferred_element_type=jnp.float32)
        return ((d_key, d_value), d_query)

    empty = jnp.zeros((total, heads, HEAD_DIM), jnp.float32)
    (d_knorm, d_value32), d_query_blocks = lax.scan(
        backward_block, (empty, empty), (probs_all, jnp.arange(blocks, dtype=jnp.int32))
    )
    d_qnorm = d_query_blocks.reshape(total, heads, HEAD_DIM)
    query_grad, q_gain_part = norm_back(q_unit, q_inv, query_gain, d_qnorm)
    key_grad, k_gain_part = norm_back(k_unit, k_inv, key_gain, d_knorm)
    value_grad = d_value32.astype(jnp.bfloat16)
    query_back, key_back, value_back = (
        lax.all_to_all(
            query_grad.reshape(total, width), "seq", split_axis=0, concat_axis=1, tiled=True
        ),
        lax.all_to_all(
            key_grad.reshape(total, width), "seq", split_axis=0, concat_axis=1, tiled=True
        ),
        lax.all_to_all(
            value_grad.reshape(total, width), "seq", split_axis=0, concat_axis=1, tiled=True
        ),
    )
    weight_shard = lax.psum_scatter(
        weight_part.astype(jnp.bfloat16), DP, scatter_dimension=1, tiled=True
    ).astype(jnp.float32)
    local_squares = jnp.sum(weight_shard * weight_shard)
    qgain_raw, kgain_raw = (
        one_axis_at_a_time(q_gain_part, DP_SEQ),
        one_axis_at_a_time(k_gain_part, DP_SEQ),
    )
    weight_squares = one_axis_at_a_time(local_squares, DP_SEQ)
    squares = weight_squares + jnp.sum(qgain_raw * qgain_raw) + jnp.sum(kgain_raw * kgain_raw)
    grad_norm = jnp.sqrt(squares)
    factor = jnp.minimum(jnp.float32(1.0), MAX_NORM / (grad_norm + EPS))
    return (
        query_back[None],
        key_back[None],
        value_back[None],
        weight_shard * factor,
        qgain_raw * factor,
        kgain_raw * factor,
        grad_norm,
    )


def solution(mesh):
    torus = Mesh(mesh.devices.reshape(4, 4, 2, mesh.shape["seq"]), ("dp_0", "dp_1", "dp_2", "seq"))
    return jax.shard_map(
        local,
        mesh=torus,
        in_specs=(
            P(DP, "seq", None),
            P(DP, "seq", None),
            P(DP, "seq", None),
            P(DP, "seq", None),
            P(DP, None),
            P("seq", None),
            P(),
            P(),
        ),
        out_specs=(
            P(DP, "seq", None),
            P(DP, "seq", None),
            P(DP, "seq", None),
            P("seq", DP),
            P(),
            P(),
            P(),
        ),
        check_vma=False,
    )
```

profile of v0, /device:TPU:1, one launch (start us, length us, event | category | flops | bytes accessed | tf_op | source)
XLA Modules:
  0.0 428.3 jit_solution(6281215837916845542)
XLA Ops:
  9.5 9.0 %all-to-all-start = ((bf16[128,8,384]{0,2,1:T(8,128)(2,1)}), bf16[128,8,384]{0,2,1:T(8,128)(2,1)S(1)}, u32[]{:S(2)}, u32[]{:S(2)}) async-start(bf16[128,8,384]{0,2,1:T(8,128)(2,1)} %bitcast.4), calls=%async_computation | async-start | bytes 1572864 | tf_op jit(solution)/shard_map/all_to_all | solution.py:46
  19.6 28.8 %all-to-all-done = bf16[128,8,384]{0,2,1:T(8,128)(2,1)S(1)} async-done(((bf16[128,8,384]{0,2,1:T(8,128)(2,1)}), bf16[128,8,384]{0,2,1:T(8,128)(2,1)S(1)}, u32[]{:S(2)}, u32[]{:S(2)}) %all-to-all-start) | async-done | bytes 786464 | tf_op jit(solution)/shard_map/all_to_all | solution.py:46
  48.4 3.5 all-to-all-start.1
  53.2 30.4 %all-to-all-done.1 = bf16[128,8,384]{0,2,1:T(8,128)(2,1)S(1)} async-done(((bf16[128,8,384]{0,2,1:T(8,128)(2,1)}), bf16[128,8,384]{0,2,1:T(8,128)(2,1)S(1)}, u32[]{:S(2)}, u32[]{:S(2)}) %all-to-all-start.1) | async-done | bytes 786464 | tf_op jit(solution)/shard_map/all_to_all | solution.py:47
  83.6 4.2 all-to-all-start.2
  89.3 1.6 reshape.182
  91.0 1.3 convert_bitcast_fusion
  92.2 2.1 copy.147
  94.3 1.5 reshape.183
  97.6 2.3 copy.151
  99.9 19.3 %all-to-all-done.2 = bf16[128,8,384]{0,2,1:T(8,128)(2,1)} async-done(((bf16[128,8,384]{0,2,1:T(8,128)(2,1)}), bf16[128,8,384]{0,2,1:T(8,128)(2,1)}, u32[]{:S(2)}, u32[]{:S(2)}) %all-to-all-start.2) | async-done | bytes 786464 | tf_op jit(solution)/shard_map/all_to_all | solution.py:48
  119.2 2.5 copy.149
  121.7 2.2 reshape.177
  123.9 2.3 copy.152
  126.2 1.7 multiply_reduce_fusion.5
  129.2 21.1 %while.27 = (s32[]{:T(128)}, bf16[2,3,512,1024]{3,2,1,0:T(8,128)(2,1)}, bf16[2,512,3,128]{3,1,2,0:T(8,128)(2,1)}, s32[2]{0:T(128)S(1)}, s32[1024]{0:T(1024)S(1)}...) while((s32[]{:T(128)}, ...), condition=%wide.region_6.7_spmd, body=%wide.region_4.6_spmd.sunk | while | flops 817035776 | bytes 85746000 | solution.py:75
  130.9 3.4 fusion.75
  134.4 1.9 bitcast_dynamic-update-slice_fusion.2
  137.4 1.5 copy-done.1
  141.5 3.4 fusion.75
  145.0 1.9 bitcast_dynamic-update-slice_fusion.2
  148.0 1.5 copy-done.1
  150.4 3.1 copy.167
  153.5 2.2 copy.180
  155.8 1.5 copy.176
  157.3 34.3 %all-gather.3.cloned.1.call-done = bf16[1,1024,6144]{2,1,0:T(8,128)(2,1)} async-done(((bf16[1,128,6144]{2,1,0:T(8,128)(2,1)}), bf16[1,1024,6144]{2,1,0:T(8,128)(2,1)}) %all-gather.3.cloned.1.call-update) | async-done | bytes 12582928 | tf_op jit(solution)/shard_map/all_gather | solution.py:77
  191.6 11.4 %fusion.42 = bf16[384,6144]{0,1:T(8,128)(2,1)} fusion(bf16[1024,384]{0,1:T(8,128)(2,1)} %bitcast.161, bf16[1,1024,6144]{2,1,0:T(8,128)(2,1)} %all-gather.3.cloned.1.call-done), kind=kOutput, calls=%fused_computation.45 | convolution fusion | flops 4834197504 | bytes 18087936 | tf_op jit(solution)/shard_map/dot_general | solution.py:78
  203.0 10.4 %fusion.48 = bf16[1024,384]{0,1:T(8,128)(2,1)} fusion(bf16[384,6144]{1,0:T(8,128)(2,1)} %param.17, bf16[1,1024,6144]{2,1,0:T(8,128)(2,1)} %all-gather.3.cloned.1.call-done), kind=kOutput, calls=%fused_computation.62 | convolution fusion | flops 4832231424 | bytes 18087936 | tf_op jit(solution)/shard_map/dot_general | solution.py:79
  213.4 58.2 %while.28 = (s32[]{:T(128)}, f32[1024,3,128]{0,2,1:T(8,128)}, f32[1024,3,128]{0,2,1:T(8,128)S(1)}, f32[2,512,3,128]{3,1,2,0:T(8,128)}, s32[2]{0:T(128)S(1)}, /*i...) while((s32[]{:T(128)}, f32[1024,3,128]{0,2,1:T(8,128)}, ...), condition=%wide.region_9.10_spmd.clone, body=%wide.region_7.9_spmd.clone.sunk | while | flops 1634210816 | bytes 57019604 | solution.py:104
  214.6 5.0 %fusion.83 = f32[3,512,1024]{2,1,0:T(8,128)} fusion(bf16[1024,3,128]{2,0,1:T(8,128)(2,1)} %get-tuple-element.549, bf16[1024,3,128]{0,2,1:T(8,128)(2,1)} %get-tuple-element.548, s32[]{:T(128)S(6)} %select_n.24), kind=kOutput, calls=%fused_computation.30.clone.1 | convolution fusion | flops 402653184 | bytes 7471108 | tf_op jit(solution)/shard_map/while/body/eval_jaxpr/qhd,khd->hqk/dot_general | solution.py:90
  219.6 10.2 %bitcast_add_fusion.4 = f32[1024,3,128]{0,2,1:T(8,128)} fusion(f32[1024,3,128]{0,2,1:T(8,128)} %get-tuple-element.528, f32[3,512,1024]{2,1,0:T(8,128)} %fusion.83, bf16[2,3,512,1024]{3,2,1,0:T(8,128)(2,1)} %get-tuple-element.547, s32[]{:T(128)} %get-tuple-element.527, pred[]{:T(512)S(6)} %compare.3, bf16[1024,3,128]{0,2,1:T(8,128)(2,1)} %get-tuple-element.546, ...), kind=kOutput, calls=%fused_computation.26.clone.1 | convolution fusion | flops 414452224 | bytes 22414340 | tf_op jit(solution)/shard_map/while/body/eval_jaxpr/hqk,qhd->khd/dot_general | solution.py:97
  229.8 9.7 %fusion.84 = f32[2,512,3,128]{3,1,2,0:T(8,128)} fusion(f32[2,512,3,128]{3,1,2,0:T(8,128)} %get-tuple-element.530, s32[]{:T(128)} %get-tuple-element.527, bf16[1024,3,128]{2,0,1:T(8,128)(2,1)} %get-tuple-element.550, f32[3,512,1024]{2,1,0:T(8,128)} %fusion.83, bf16[2,3,512,1024]{3,2,1,0:T(8,128)(2,1)} %get-tuple-element.547), kind=kOutput, calls=%fused_computation.28.clone.1 | convolution fusion | flops 413665792 | bytes 20448768 | tf_op jit(solution)/shard_map/while/body/eval_jaxpr/hqk,khd->qhd/dot_general | solution.py:100
  239.5 3.0 bitcast_add_fusion.5
  243.8 4.9 %fusion.83 = f32[3,512,1024]{2,1,0:T(8,128)} fusion(bf16[1024,3,128]{2,0,1:T(8,128)(2,1)} %get-tuple-element.549, bf16[1024,3,128]{0,2,1:T(8,128)(2,1)} %get-tuple-element.548, s32[]{:T(128)S(6)} %select_n.24), kind=kOutput, calls=%fused_computation.30.clone.1 | convolution fusion | flops 402653184 | bytes 7471108 | tf_op jit(solution)/shard_map/while/body/eval_jaxpr/qhd,khd->hqk/dot_general | solution.py:90
  248.7 10.5 %bitcast_add_fusion.4 = f32[1024,3,128]{0,2,1:T(8,128)} fusion(f32[1024,3,128]{0,2,1:T(8,128)} %get-tuple-element.528, f32[3,512,1024]{2,1,0:T(8,128)} %fusion.83, bf16[2,3,512,1024]{3,2,1,0:T(8,128)(2,1)} %get-tuple-element.547, s32[]{:T(128)} %get-tuple-element.527, pred[]{:T(512)S(6)} %compare.3, bf16[1024,3,128]{0,2,1:T(8,128)(2,1)} %get-tuple-element.546, ...), kind=kOutput, calls=%fused_computation.26.clone.1 | convolution fusion | flops 414452224 | bytes 22414340 | tf_op jit(solution)/shard_map/while/body/eval_jaxpr/hqk,qhd->khd/dot_general | solution.py:97
  259.2 9.4 %fusion.84 = f32[2,512,3,128]{3,1,2,0:T(8,128)} fusion(f32[2,512,3,128]{3,1,2,0:T(8,128)} %get-tuple-element.530, s32[]{:T(128)} %get-tuple-element.527, bf16[1024,3,128]{2,0,1:T(8,128)(2,1)} %get-tuple-element.550, f32[3,512,1024]{2,1,0:T(8,128)} %fusion.83, bf16[2,3,512,1024]{3,2,1,0:T(8,128)(2,1)} %get-tuple-element.547), kind=kOutput, calls=%fused_computation.28.clone.1 | convolution fusion | flops 413665792 | bytes 20448768 | tf_op jit(solution)/shard_map/while/body/eval_jaxpr/hqk,khd->qhd/dot_general | solution.py:100
  268.6 2.9 bitcast_add_fusion.5
  271.6 3.7 copy.156
  275.3 2.7 copy.159
  277.9 3.0 copy.160
  280.9 2.3 multiply_reduce_fusion.3
  283.4 1.6 copy.177
  285.0 3.3 reshape.179
  288.3 4.3 fusion.47
  292.6 4.5 %all-to-all-start.3 = ((bf16[8,128,384]{1,2,0:T(8,128)(2,1)}), bf16[8,128,384]{1,2,0:T(8,128)(2,1)}, u32[]{:S(2)}, u32[]{:S(2)}) async-start(bf16[8,128,384]{1,2,0:T(8,128)(2,1)} %fusion.47), calls=%async_computation.3 | async-start | bytes 1572864 | tf_op jit(solution)/shard_map/all_to_all | solution.py:112
  297.1 2.0 multiply_reduce_fusion
  299.8 1.4 copy.163
  301.1 17.6 %all-to-all-done.3 = bf16[8,128,384]{1,2,0:T(8,128)(2,1)} async-done(((bf16[8,128,384]{1,2,0:T(8,128)(2,1)}), bf16[8,128,384]{1,2,0:T(8,128)(2,1)}, u32[]{:S(2)}, u32[]{:S(2)}) %all-to-all-start.3) | async-done | bytes 786464 | tf_op jit(solution)/shard_map/all_to_all | solution.py:112
  318.7 3.5 all-to-all-start.4
  322.6 1.4 copy.165
  324.0 20.0 %all-to-all-done.4 = bf16[8,128,384]{2,1,0:T(8,128)(2,1)S(1)} async-done(((bf16[8,128,384]{2,1,0:T(8,128)(2,1)}), bf16[8,128,384]{2,1,0:T(8,128)(2,1)S(1)}, u32[]{:S(2)}, u32[]{:S(2)}) %all-to-all-start.4) | async-done | bytes 786464 | tf_op jit(solution)/shard_map/all_to_all | solution.py:115
  343.9 4.2 all-to-all-start.5
  348.2 1.9 reshape.184
  350.1 2.6 multiply_reduce_fusion.1
  352.8 2.4 copy.170
  355.5 1.2 copy.171
  356.7 13.2 %all-to-all-done.5 = bf16[8,128,384]{2,1,0:T(8,128)(2,1)} async-done(((bf16[8,128,384]{2,1,0:T(8,128)(2,1)}), bf16[8,128,384]{2,1,0:T(8,128)(2,1)}, u32[]{:S(2)}, u32[]{:S(2)}) %all-to-all-start.5) | async-done | bytes 786464 | tf_op jit(solution)/shard_map/all_to_all | solution.py:118
  369.8 1.5 copy.166
  372.5 1.6 fusion.51
  374.1 13.1 %all-reduce.2 = (f32[]{:T(128)}, f32[128]{0:T(128)S(1)}, f32[128]{0:T(128)S(1)}) all-reduce(f32[]{:T(128)} %fusion.51, f32[128]{0:T(128)S(1)} %multiply_reduce_fusion.1, f32[128]{0:T(128)S(1)} %get-tuple-element.303), channel_id=1, replica_groups=mesh['dp_0'=4,'dp_1'=4,'dp_2'=2,'seq'=8] {'dp_0'}, use_global_device_ids=true, to_apply=%region_14.15 | all-reduce | flops 257 | bytes 2056 | tf_op jit(solution)/shard_map/psum | solution.py:18
  387.2 9.2 %all-reduce.1 = (f32[]{:T(128)}, f32[128]{0:T(128)S(1)}, f32[128]{0:T(128)S(1)}) all-reduce(f32[]{:T(128)} %get-tuple-element.347, f32[128]{0:T(128)S(1)} %get-tuple-element.348, f32[128]{0:T(128)S(1)} %get-tuple-element.349), channel_id=1, replica_groups=mesh['dp_0'=4,'dp_1'=4,'dp_2'=2,'seq'=8] {'dp_1'}, use_global_device_ids=true, to_apply=%region_15.16 | all-reduce | flops 257 | bytes 2056 | tf_op jit(solution)/shard_map/psum | solution.py:18
  396.4 7.1 %all-reduce.3 = (f32[]{:T(128)}, f32[128]{0:T(128)S(1)}, f32[128]{0:T(128)S(1)}) all-reduce(f32[]{:T(128)} %get-tuple-element.344, f32[128]{0:T(128)S(1)} %get-tuple-element.345, f32[128]{0:T(128)S(1)} %get-tuple-element.346), channel_id=1, replica_groups=mesh['dp_0'=4,'dp_1'=4,'dp_2'=2,'seq'=8] {'dp_2'}, use_global_device_ids=true, to_apply=%region_16.17 | all-reduce | flops 257 | bytes 2056 | tf_op jit(solution)/shard_map/psum | solution.py:18
  403.5 11.6 %all-reduce = (f32[]{:T(128)}, f32[128]{0:T(128)S(1)}, f32[128]{0:T(128)S(1)}) all-reduce(f32[]{:T(128)} %get-tuple-element.350, f32[128]{0:T(128)S(1)} %get-tuple-element.351, f32[128]{0:T(128)S(1)} %get-tuple-element.352), channel_id=1, replica_groups=mesh['dp_0'=4,'dp_1'=4,'dp_2'=2,'seq'=8] {'seq'}, use_global_device_ids=true, to_apply=%region_17.18 | all-reduce | flops 257 | bytes 2056 | tf_op jit(solution)/shard_map/psum | solution.py:18
  418.7 1.6 convert_multiply_fusion.15
  (97 shorter events, 20.8 us)
Async XLA Ops:
  7.2 1.1 copy-start.12
  7.2 184.4 %all-gather.3.cloned.1.call-start = ((), (), s32[]{:S(2)}) async-start(), calls=%async_computation.8 | async-start | bytes 14155776 | tf_op jit(solution)/shard_map/all_gather | solution.py:77
  8.3 10.2 %copy-start.13 = (bf16[1,128,3072]{2,1,0:T(8,128)(2,1)S(1)}, bf16[1,128,3072]{2,1,0:T(8,128)(2,1)}, u32[]{:S(2)}) copy-start(bf16[1,128,3072]{2,1,0:T(8,128)(2,1)} %param.13) | copy-start | bytes 2359300
  9.5 39.0 %all-to-all-start = ((bf16[128,8,384]{0,2,1:T(8,128)(2,1)}), bf16[128,8,384]{0,2,1:T(8,128)(2,1)S(1)}, u32[]{:S(2)}, u32[]{:S(2)}) async-start(bf16[128,8,384]{0,2,1:T(8,128)(2,1)} %bitcast.4), calls=%async_computation | async-start | bytes 1572864 | tf_op jit(solution)/shard_map/all_to_all | solution.py:46
  18.5 33.5 %copy-start.14 = (bf16[1,128,3072]{2,1,0:T(8,128)(2,1)S(1)}, bf16[1,128,3072]{2,1,0:T(8,128)(2,1)}, u32[]{:S(2)}) copy-start(bf16[1,128,3072]{2,1,0:T(8,128)(2,1)} %param.14) | copy-start | bytes 2359300
  48.4 39.8 %copy-start.7 = (bf16[128,8,384]{0,2,1:T(8,128)(2,1)}, bf16[128,8,384]{0,2,1:T(8,128)(2,1)S(1)}, u32[]{:S(2)}) copy-start(bf16[128,8,384]{0,2,1:T(8,128)(2,1)S(1)} %all-to-all-done) | copy-start | bytes 2359300
  48.4 35.2 %all-to-all-start.1 = ((bf16[128,8,384]{0,2,1:T(8,128)(2,1)}), bf16[128,8,384]{0,2,1:T(8,128)(2,1)S(1)}, u32[]{:S(2)}, u32[]{:S(2)}) async-start(bf16[128,8,384]{0,2,1:T(8,128)(2,1)} %bitcast.8), calls=%async_computation.1 | async-start | bytes 1572864 | tf_op jit(solution)/shard_map/all_to_all | solution.py:47
  52.0 35.9 %copy-start.18 = (f32[128]{0:T(128)S(1)}, f32[128]{0:T(128)}, u32[]{:S(2)}) copy-start(f32[128]{0:T(128)} %param.18) | copy-start | bytes 1540
  52.0 35.9 %copy-start.19 = (s32[1,4]{1,0:T(1,128)S(1)}, s32[1,4]{1,0:T(1,128)}, u32[]{:S(2)}) copy-start(s32[1,4]{1,0:T(1,128)} %param.16) | copy-start | bytes 52
  83.6 4.6 %copy-start.11 = (bf16[128,8,384]{0,2,1:T(8,128)(2,1)}, bf16[128,8,384]{0,2,1:T(8,128)(2,1)S(1)}, u32[]{:S(2)}) copy-start(bf16[128,8,384]{0,2,1:T(8,128)(2,1)S(1)} %all-to-all-done.1) | copy-start | bytes 2359300
  83.6 35.6 %all-to-all-start.2 = ((bf16[128,8,384]{0,2,1:T(8,128)(2,1)}), bf16[128,8,384]{0,2,1:T(8,128)(2,1)}, u32[]{:S(2)}, u32[]{:S(2)}) async-start(bf16[128,8,384]{0,2,1:T(8,128)(2,1)} %bitcast.10), calls=%async_computation.2 | async-start | bytes 1572864 | tf_op jit(solution)/shard_map/all_to_all | solution.py:48
  87.8 284.7 %reduce-scatter.2.cloned.1.call-start = ((), (), s32[]{:S(2)}) async-start(), calls=%async_computation.7 | async-start | bytes 4866048 | tf_op jit(solution)/shard_map/reduce_scatter | solution.py:122
  89.3 1.7 copy-start.4
  95.8 0.7 copy-start.17
  126.2 1.9 copy-start.3
  130.9 3.4 copy-start
  134.4 1.9 copy-start.2
  134.4 1.9 copy-start.15
  136.3 2.6 copy-start.1
  138.9 0.9 copy-start.16
  141.5 3.5 copy-start
  145.0 1.9 copy-start.2
  145.0 1.9 copy-start.15
  146.9 2.6 copy-start.1
  149.5 0.9 copy-start.16
  292.6 26.1 %all-to-all-start.3 = ((bf16[8,128,384]{1,2,0:T(8,128)(2,1)}), bf16[8,128,384]{1,2,0:T(8,128)(2,1)}, u32[]{:S(2)}, u32[]{:S(2)}) async-start(bf16[8,128,384]{1,2,0:T(8,128)(2,1)} %fusion.47), calls=%async_computation.3 | async-start | bytes 1572864 | tf_op jit(solution)/shard_map/all_to_all | solution.py:112
  297.1 2.0 copy-start.8
  318.7 25.2 %all-to-all-start.4 = ((bf16[8,128,384]{2,1,0:T(8,128)(2,1)}), bf16[8,128,384]{2,1,0:T(8,128)(2,1)S(1)}, u32[]{:S(2)}, u32[]{:S(2)}) async-start(bf16[8,128,384]{2,1,0:T(8,128)(2,1)} %copy.163), calls=%async_computation.4 | async-start | bytes 1572864 | tf_op jit(solution)/shard_map/all_to_all | solution.py:115
  322.6 25.6 %copy-start.5 = (f32[8,128,384]{1,0,2:T(8,128)S(1)}, f32[8,128,384]{1,0,2:T(8,128)}, u32[]{:S(2)}) copy-start(f32[8,128,384]{1,0,2:T(8,128)} %copy-done.4) | copy-start | bytes 4718596
  343.9 4.2 copy-start.9
  343.9 25.9 %all-to-all-start.5 = ((bf16[8,128,384]{2,1,0:T(8,128)(2,1)}), bf16[8,128,384]{2,1,0:T(8,128)(2,1)}, u32[]{:S(2)}, u32[]{:S(2)}) async-start(bf16[8,128,384]{2,1,0:T(8,128)(2,1)} %copy.165), calls=%async_computation.5 | async-start | bytes 1572864 | tf_op jit(solution)/shard_map/all_to_all | solution.py:118
  348.2 1.9 copy-start.6
  352.8 2.4 copy-start.10
Sparse Core Ops, SparseCore 0:
  9.8 181.7 all-gather.2
  203.1 88.8 reduce-scatter.1
where the time goes:
time: 432 us; the launch traced here: 428 us
  waiting for transfers between devices  164 us (38%)
  matrix products  86.5 us (20%)
  local copies, waits for them, and re-layouts  60.2 us (14%)
  blocking collectives  40.9 us (9%)
  starting transfers between devices  29.1 us (7%)
  other arithmetic  26.9 us (6%)
  between operations  17.6 us (4%)
    psum x4, blocking collectives, one_axis_at_a_time(): array = lax.psum(array, axis)  40.9 us
    all_gather x1, waiting for transfers between devices, local(): out_full = lax.all_gather(out_grad[0], 'seq', axis=0, tiled=True)  34.3 us
    all_to_all x1, waiting for transfers between devices, local(): lax.all_to_all(key_rows[0], 'seq', split_axis=1, concat_axis=0, tiled=True)  30.4 us
    all_to_all x1, waiting for transfers between devices, local(): lax.all_to_all(query_rows[0], 'seq', split_axis=1, concat_axis=0, tiled=T...  28.8 us
    dot_general x2, matrix products, backward_block(): jnp.einsum('hqk,qhd->khd', d_scores, query_block, preferred_element_type=...  20.7 us
    all_to_all x1, waiting for transfers between devices, local(): lax.all_to_all(key_grad.reshape(total, width), 'seq', split_axis=0, conca...  20 us
    all_to_all x1, waiting for transfers between devices, local(): lax.all_to_all(value_rows[0], 'seq', split_axis=1, concat_axis=0, tiled=T...  19.3 us
    dot_general x2, matrix products, backward_block(): jnp.einsum('hqk,khd->qhd', d_scores, k_norm, preferred_element_type=jnp.f...  19.1 us
  transfers between devices with their start and end apart: 8, of which 7 were waited for; matrix products, arithmetic and copies ran while one was open for 35% of the time, Pallas kernels for 0%

commit v1 on v0

v1 whole, which is shorter than its diff:
```python
import functools

import jax
import jax.numpy as jnp
from jax import lax
from jax.experimental import pallas as pl
from jax.experimental.pallas import tpu as pltpu
from jax.sharding import Mesh
from jax.sharding import PartitionSpec as P

HEAD_DIM = 128
MAX_NORM = 768
EPS = 1e-06
DP = ("dp_0", "dp_1", "dp_2")
MESH = pl.DeviceIdType.MESH
F32 = jnp.float32
BF16 = jnp.bfloat16
NN = (((1,), (0,)), ((), ()))
NT = (((1,), (1,)), ((), ()))
SUBS = 2


def dot(a, b, dims=NN):
    return lax.dot_general(a, b, dims, preferred_element_type=F32)


def seg_of(places, ends_ref):
    seg = jnp.zeros(places.shape, jnp.int32)
    for c in range(ends_ref.shape[0]):
        seg = seg + (places >= ends_ref[c]).astype(jnp.int32)
    return seg


def attention_kernel(
    n,
    q_hbm,
    k_hbm,
    v_hbm,
    do_hbm,
    w_hbm,
    ends_ref,
    qg_ref,
    kg_ref,
    dq_out,
    dk_out,
    dv_out,
    wp_out,
    gain_out,
    qkv,
    kn,
    knt,
    vt,
    do_all,
    w,
    wacc,
    dkt,
    dvt,
    datt,
    attnt,
    dqs,
    qkv_send,
    qkv_recv,
    ag_send,
    ag_recv,
    dq_send,
    dq_recv,
    own_sem,
):
    me = lax.axis_index("seq")
    core = lax.axis_index("dp_2")
    sign = 1 - 2 * core
    tokens = q_hbm.shape[0]
    total = tokens * n
    width = q_hbm.shape[1] // n
    heads = width // HEAD_DIM
    model = do_hbm.shape[1]
    scale = HEAD_DIM ** (-0.5)
    half = tokens // SUBS
    up = lax.rem(me + sign + n, n)
    down = lax.rem(me - sign + n, n)
    a_steps = n // 2
    b_steps = n - 1 - a_steps

    def columns(index):
        return pl.ds(pl.multiple_of(index * width, width), width)

    def rows_of(index):
        return pl.ds(pl.multiple_of(index * tokens, tokens), tokens)

    def peer(d):
        return lax.rem(me + d, n)

    barrier = pltpu.get_barrier_semaphore()
    for d in range(1, n):
        pl.semaphore_signal(barrier, inc=1, device_id={"seq": peer(d)}, device_id_type=MESH)

    w_copy = pltpu.make_async_copy(w_hbm, w, own_sem.at[4])
    do_copy = pltpu.make_async_copy(do_hbm, do_all.at[me], own_sem.at[3])
    own_copies = [
        pltpu.make_async_copy(ref.at[:, columns(me)], qkv.at[i, rows_of(me)], own_sem.at[i])
        for i, ref in enumerate((q_hbm, k_hbm, v_hbm))
    ]
    for copy in own_copies + [do_copy, w_copy]:
        copy.start()
    pl.semaphore_wait(barrier, n - 1)

    def qkv_copy(i, ref, d):
        to = peer(d)
        return pltpu.make_async_remote_copy(
            src_ref=ref.at[:, columns(to)],
            dst_ref=qkv.at[i, rows_of(me)],
            send_sem=qkv_send.at[i, d],
            recv_sem=qkv_recv.at[i, me],
            device_id={"seq": to},
            device_id_type=MESH,
        )

    def qkv_arrival(i, ref, d):
        source = peer(d)
        return pltpu.make_async_remote_copy(
            src_ref=ref.at[:, columns(me)],
            dst_ref=qkv.at[i, rows_of(source)],
            send_sem=qkv_send.at[i, d],
            recv_sem=qkv_recv.at[i, source],
            device_id={"seq": source},
            device_id_type=MESH,
        )

    order = [4, 3, 5, 2, 6, 1, 7] if n == 8 else list(range(1, n))
    arrays = ((1, k_hbm), (2, v_hbm), (0, q_hbm))
    for i, ref in arrays:
        for d in order:
            qkv_copy(i, ref, d).start()

    def ring(direction, step, sub, block, to, source=None):
        piece = pl.ds(sub * half, half)
        return pltpu.make_async_remote_copy(
            src_ref=do_all.at[block, piece] if source is None else source.at[piece],
            dst_ref=do_all.at[block, piece],
            send_sem=ag_send.at[direction, step, sub],
            recv_sem=ag_recv.at[block, sub],
            device_id={"seq": to},
            device_id_type=MESH,
        )

    for sub in range(SUBS):
        ring(0, 0, sub, me, up, do_hbm).start()
        ring(1, 0, sub, me, down, do_hbm).start()

    dkt[...] = jnp.zeros(dkt.shape, F32)
    dvt[...] = jnp.zeros(dvt.shape, F32)
    gain_out[...] = jnp.zeros(gain_out.shape, F32)

    def clear(i, carry):
        wacc[:, pl.ds(pl.multiple_of(i * 512, 512), 512)] = jnp.zeros((width, 512), F32)
        return carry

    lax.fori_loop(0, model // 512, clear, 0)

    for copy in own_copies:
        copy.wait()
    for i, ref in arrays:
        for d in range(1, n):
            qkv_arrival(i, ref, d).wait_recv()

    kg = kg_ref[...]
    qg = qg_ref[...]
    for h in range(heads):
        cols = pl.ds(h * HEAD_DIM, HEAD_DIM)

        def prepare(j, carry, cols=cols):
            rows = pl.ds(pl.multiple_of(j * 256, 256), 256)
            keys = qkv[1, rows, cols].astype(F32)
            inverse = lax.rsqrt(jnp.mean(keys * keys, axis=-1, keepdims=True) + EPS)
            normed = keys * inverse * kg
            kn[rows, cols] = normed.astype(BF16)
            knt[cols, rows] = jnp.transpose(normed).astype(BF16)
            vt[cols, rows] = jnp.transpose(qkv[2, rows, cols].astype(F32)).astype(BF16)
            return carry

        lax.fori_loop(0, total // 256, prepare, 0)

    seg_k = seg_of(lax.broadcasted_iota(jnp.int32, (1, total), 1), ends_ref)
    do_copy.wait()
    w_copy.wait()

    def dq_copy(t):
        return pltpu.make_async_remote_copy(
            src_ref=dqs.at[t],
            dst_ref=dq_out.at[:, columns(me)],
            send_sem=dq_send.at[t],
            recv_sem=dq_recv.at[me],
            device_id={"seq": t},
            device_id_type=MESH,
        )

    def body(i, carry):
        step = (i + 1) // 2
        odd = lax.rem(i, 2)
        shift = sign * step
        t = lax.rem(me + shift - 2 * odd * shift + n, n)
        a_block = lax.rem(me - shift + n, n)
        b_block = lax.rem(me + shift + n, n)

        @pl.when(odd == 1)
        def _():
            for sub in range(SUBS):
                ring(0, step - 1, sub, a_block, up).wait_recv()

                @pl.when(step < a_steps)
                def _():
                    ring(0, step, sub, a_block, up).start()

            @pl.when(step <= b_steps)
            def _():
                for sub in range(SUBS):
                    ring(1, step - 1, sub, b_block, down).wait_recv()

                    @pl.when(step < b_steps)
                    def _():
                        ring(1, step, sub, b_block, down).start()

        datt[...] = jnp.zeros(datt.shape, F32)

        def project(j, c):
            part = pl.ds(pl.multiple_of(j * 1024, 1024), 1024)
            datt[...] += dot(do_all[t, :, part], w[:, part], NT)
            return c

        lax.fori_loop(0, model // 1024, project, 0)
        rows = rows_of(t)
        places = lax.broadcasted_iota(jnp.int32, (tokens, 1), 0) + t * tokens
        same = seg_of(places, ends_ref) == seg_k
        gain = jnp.zeros((1, HEAD_DIM), F32)
        for h in range(heads):
            cols = pl.ds(h * HEAD_DIM, HEAD_DIM)
            query = qkv[0, rows, cols].astype(F32)
            inverse = lax.rsqrt(jnp.mean(query * query, axis=-1, keepdims=True) + EPS)
            unit = query * inverse
            normed = unit * qg
            qn = normed.astype(BF16)
            expo = jnp.where(same, jnp.exp(dot(qn, knt[cols, :]) * scale), 0.0)
            probs = (expo * (1.0 / jnp.sum(expo, axis=-1, keepdims=True))).astype(BF16)
            attn = dot(probs, qkv[2, :, cols])
            attnt[cols, :] = jnp.transpose(attn).astype(BF16)
            dattn = datt[:, cols]
            d_probs = dot(dattn.astype(BF16), vt[cols, :])
            probs32 = probs.astype(F32)
            row_sum = jnp.sum(probs32 * d_probs, axis=-1, keepdims=True)
            d_scores = (probs32 * (d_probs - row_sum) * scale).astype(BF16)
            dvt[cols, :] += dot(jnp.transpose(dattn).astype(BF16), probs)
            dkt[cols, :] += dot(jnp.transpose(normed).astype(BF16), d_scores)
            d_normed = dot(d_scores, kn[:, cols])
            gain = gain + jnp.sum(unit * d_normed, axis=0, keepdims=True)
            d_unit = d_normed * qg
            d_query = inverse * (d_unit - unit * jnp.mean(unit * d_unit, axis=-1, keepdims=True))
            dqs[t, :, cols] = d_query.astype(BF16)
        gain_out[0:1, :] += gain

        @pl.when(i > 0)
        def _():
            dq_copy(t).start()

        def weigh(j, c):
            part = pl.ds(pl.multiple_of(j * 512, 512), 512)
            wacc[:, part] += dot(attnt[...], do_all[t, :, part])
            return c

        lax.fori_loop(0, model // 512, weigh, 0)
        return carry

    lax.fori_loop(0, n, body, 0)

    own_dq = pltpu.make_async_copy(dqs.at[me], dq_out.at[:, columns(me)], own_sem.at[0])
    own_dq.start()

    for h in range(heads):
        cols = pl.ds(h * HEAD_DIM, HEAD_DIM)

        def finish(j, gain, cols=cols):
            rows = pl.ds(pl.multiple_of(j * 256, 256), 256)
            keys = qkv[1, rows, cols].astype(F32)
            inverse = lax.rsqrt(jnp.mean(keys * keys, axis=-1, keepdims=True) + EPS)
            unit = keys * inverse
            d_normed = jnp.transpose(dkt[cols, rows])
            d_unit = d_normed * kg
            d_key = inverse * (d_unit - unit * jnp.mean(unit * d_unit, axis=-1, keepdims=True))
            dk_out[rows, cols] = d_key.astype(BF16)
            dv_out[rows, cols] = jnp.transpose(dvt[cols, rows]).astype(BF16)
            return gain + jnp.sum(unit * d_normed, axis=0, keepdims=True)

        gain = lax.fori_loop(0, total // 256, finish, jnp.zeros((1, HEAD_DIM), F32))
        gain_out[1:2, :] += gain

    def narrow(i, carry):
        part = pl.ds(pl.multiple_of(i * 512, 512), 512)
        wp_out[:, part] = wacc[:, part].astype(BF16)
        return carry

    lax.fori_loop(0, model // 512, narrow, 0)

    own_dq.wait()
    for i, ref in arrays:
        for d in order:
            qkv_copy(i, ref, d).wait_send()
    for sub in range(SUBS):
        for step in range(a_steps):
            ring(0, step, sub, me, up).wait_send()
        for step in range(b_steps):
            ring(1, step, sub, me, down).wait_send()
    for d in range(1, n):
        dq_copy(peer(d)).wait_send()
        source = peer(d)
        pltpu.make_async_remote_copy(
            src_ref=dqs.at[source],
            dst_ref=dq_out.at[:, columns(source)],
            send_sem=dq_send.at[source],
            recv_sem=dq_recv.at[source],
            device_id={"seq": source},
            device_id_type=MESH,
        ).wait_recv()


def exchange_kernel(
    n,
    side,
    dk_ref,
    dv_ref,
    wp_ref,
    dk_out,
    dv_out,
    sum_out,
    mine,
    theirs,
    packed,
    slots,
    reduced,
    final,
    z_send,
    z_recv,
    c_send,
    c_recv,
    x_send,
    x_recv,
    own_sem,
):
    me = lax.axis_index("seq")
    y, x, core = (lax.axis_index(name) for name in DP)
    other = 1 - core
    tokens = dk_out.shape[0]
    width = dk_ref.shape[1]
    rows_half = wp_ref.shape[0] // 2
    chips = side * side
    chunk = wp_ref.shape[1] // chips
    here = y * side + x

    def peer(d):
        return lax.rem(me + d, n)

    def columns(index):
        return pl.ds(pl.multiple_of(index * width, width), width)

    def rows_of(index):
        return pl.ds(pl.multiple_of(index * tokens, tokens), tokens)

    def chunk_of(index):
        return pl.ds(pl.multiple_of(index * chunk, chunk), chunk)

    def chip(d):
        place = lax.rem(here + d, chips)
        return {"dp_0": place // side, "dp_1": lax.rem(place, side)}, place

    barrier = pltpu.get_barrier_semaphore()
    for d in range(1, n):
        pl.semaphore_signal(barrier, inc=1, device_id={"seq": peer(d)}, device_id_type=MESH)
    for d in range(1, chips):
        pl.semaphore_signal(barrier, inc=1, device_id=chip(d)[0], device_id_type=MESH)
    pl.semaphore_signal(barrier, inc=1, device_id={"dp_2": other}, device_id_type=MESH)
    half_of = lambda c: pl.ds(pl.multiple_of(c * rows_half, rows_half), rows_half)
    mine_copy = pltpu.make_async_copy(wp_ref.at[half_of(core)], mine, own_sem.at[0])
    own = [
        pltpu.make_async_copy(ref.at[rows_of(me)], out.at[:, columns(me)], own_sem.at[1 + i])
        for i, (ref, out) in enumerate(((dk_ref, dk_out), (dv_ref, dv_out)))
    ]
    for copy in [mine_copy] + own:
        copy.start()
    pl.semaphore_wait(barrier, n + chips - 1)

    swap = pltpu.make_async_remote_copy(
        src_ref=wp_ref.at[half_of(other)],
        dst_ref=theirs,
        send_sem=c_send.at[0],
        recv_sem=c_recv.at[0],
        device_id={"dp_2": other},
        device_id_type=MESH,
    )
    swap.start()

    def back(i, ref, out, d, place):
        to = peer(d)
        return pltpu.make_async_remote_copy(
            src_ref=ref.at[rows_of(to)],
            dst_ref=out.at[:, columns(place)],
            send_sem=z_send.at[i, d],
            recv_sem=z_recv.at[i, place],
            device_id={"seq": to},
            device_id_type=MESH,
        )

    order = [4, 3, 5, 2, 6, 1, 7] if n == 8 else list(range(1, n))
    for i, (ref, out) in enumerate(((dk_ref, dk_out), (dv_ref, dv_out))):
        for d in order:
            back(i, ref, out, d, me).start()

    mine_copy.wait()
    swap.wait_recv()

    def merge(i, carry):
        part = chunk_of(i)
        packed[i] = (mine[:, part].astype(F32) + theirs[:, part].astype(F32)).astype(BF16)
        return carry

    lax.fori_loop(0, chips, merge, 0)

    def scatter(d, place_here):
        target, place = chip(d)
        return pltpu.make_async_remote_copy(
            src_ref=packed.at[place],
            dst_ref=slots.at[place_here],
            send_sem=x_send.at[d],
            recv_sem=x_recv.at[place_here],
            device_id=target,
            device_id_type=MESH,
        )

    for d in range(1, chips):
        scatter(d, here).start()
    reduced[...] = packed[here].astype(F32)
    for d in range(1, chips):
        place = chip(d)[1]
        scatter(d, place).wait_recv()
        reduced[...] += slots[place].astype(F32)

    window = pl.ds(pl.multiple_of(other * 128, 128), 256)
    last = pltpu.make_async_remote_copy(
        src_ref=reduced.at[:, window],
        dst_ref=final,
        send_sem=c_send.at[1],
        recv_sem=c_recv.at[1],
        device_id={"dp_2": other},
        device_id_type=MESH,
    )
    last.start()

    def pick(block):
        return jnp.where(core == 0, block[:, :192], block[:, 64:256])

    sum_out[half_of(core), :] = pick(reduced[:, pl.ds(pl.multiple_of(core * 128, 128), 256)])
    last.wait_recv()
    sum_out[half_of(other), :] = pick(final[...])
    last.wait_send()
    swap.wait_send()
    for d in range(1, chips):
        scatter(d, here).wait_send()
    for copy in own:
        copy.wait()
    for i, (ref, out) in enumerate(((dk_ref, dk_out), (dv_ref, dv_out))):
        for d in range(1, n):
            back(i, ref, out, d, me).wait_send()
            back(i, ref, out, d, peer(d)).wait_recv()


def norm_kernel(
    n,
    side,
    shard_ref,
    gain_ref,
    w_out,
    gain_out,
    norm_out,
    z_slots,
    dp_slots,
    z_send,
    z_recv,
    dp_send,
    dp_recv,
):
    me = lax.axis_index("seq")
    y, x, core = (lax.axis_index(name) for name in DP)
    group = 2 * side * side
    here = (y * side + x) * 2 + core

    def z_peer(d):
        return {"seq": lax.rem(me + d, n)}, lax.rem(me + d, n)

    def dp_peer(d):
        place = lax.rem(here + d, group)
        return {
            "dp_0": place // (2 * side),
            "dp_1": lax.rem(place // 2, side),
            "dp_2": lax.rem(place, 2),
        }, place

    barrier = pltpu.get_barrier_semaphore()
    for d in range(1, n):
        pl.semaphore_signal(barrier, inc=1, device_id=z_peer(d)[0], device_id_type=MESH)
    for d in range(1, group):
        pl.semaphore_signal(barrier, inc=1, device_id=dp_peer(d)[0], device_id_type=MESH)

    shard = shard_ref[...]
    square = jnp.sum(shard * shard)
    row = lax.broadcasted_iota(jnp.int32, (8, 128), 0)
    z_slots[me] = jnp.where(row == 2, square, gain_ref[...])
    pl.semaphore_wait(barrier, n + group - 2)

    def spread(slots, peer, count, sends, recvs, place):
        def send(d):
            return pltpu.make_async_remote_copy(
                src_ref=slots.at[place],
                dst_ref=slots.at[place],
                send_sem=sends.at[d],
                recv_sem=recvs.at[place],
                device_id=peer(d)[0],
                device_id_type=MESH,
            )

        def arrive(d):
            target, source = peer(d)
            return pltpu.make_async_remote_copy(
                src_ref=slots.at[source],
                dst_ref=slots.at[source],
                send_sem=sends.at[d],
                recv_sem=recvs.at[source],
                device_id=target,
                device_id_type=MESH,
            )

        for d in range(1, count):
            send(d).start()
        for d in range(1, count):
            arrive(d).wait_recv()
        for d in range(1, count):
            send(d).wait_send()
        total = slots[0]
        for place in range(1, count):
            total = total + slots[place]
        return total

    dp_slots[here] = spread(z_slots, z_peer, n, z_send, z_recv, me)
    total = spread(dp_slots, dp_peer, group, dp_send, dp_recv, here)
    gains = jnp.where(row < 2, total, 0.0)
    squares = jnp.sum(total[2:3, 0:1]) + jnp.sum(gains * gains)
    norm = jnp.sqrt(jnp.full((8, 128), squares, F32))
    factor = jnp.minimum(1.0, MAX_NORM / (norm + EPS))
    gain_out[...] = gains * factor
    norm_out[...] = norm
    w_out[...] = shard * factor[0:1, 0:1]


def local(n, side, query_rows, key_rows, value_rows, out_grad, clip_lengths, out_weight, query_gain, key_gain):
    tokens, inner = query_rows.shape[1:]
    model = out_grad.shape[2]
    width = inner // n
    total = tokens * n
    ends = jnp.cumsum(clip_lengths[0])
    vmem = pl.BlockSpec(memory_space=pltpu.VMEM)
    smem = pl.BlockSpec(memory_space=pltpu.SMEM)
    anywhere = pl.BlockSpec(memory_space=pl.ANY)
    dma = pltpu.SemaphoreType.DMA
    struct = jax.ShapeDtypeStruct
    chips = side * side
    dq, dk, dv, wp, gain = pl.pallas_call(
        functools.partial(attention_kernel, n),
        out_shape=(
            struct((tokens, inner), BF16),
            struct((total, width), BF16),
            struct((total, width), BF16),
            struct((width, model), BF16),
            struct((8, HEAD_DIM), F32),
        ),
        in_specs=[anywhere] * 5 + [smem, vmem, vmem],
        out_specs=(anywhere, vmem, vmem, vmem, vmem),
        scratch_shapes=[
            pltpu.VMEM((3, total, width), BF16),
            pltpu.VMEM((total, width), BF16),
            pltpu.VMEM((width, total), BF16),
            pltpu.VMEM((width, total), BF16),
            pltpu.VMEM((n, tokens, model), BF16),
            pltpu.VMEM((width, model), BF16),
            pltpu.VMEM((width, model), F32),
            pltpu.VMEM((width, total), F32),
            pltpu.VMEM((width, total), F32),
            pltpu.VMEM((tokens, width), F32),
            pltpu.VMEM((width, tokens), BF16),
            pltpu.VMEM((n, tokens, width), BF16),
            dma((3, n)),
            dma((3, n)),
            dma((2, n // 2, SUBS)),
            dma((n, SUBS)),
            dma((n,)),
            dma((n,)),
            dma((5,)),
        ],
        compiler_params=pltpu.CompilerParams(
            collective_id=1, has_side_effects=True, vmem_limit_bytes=60 * 1024 * 1024
        ),
        name="attention",
    )(
        query_rows[0],
        key_rows[0],
        value_rows[0],
        out_grad[0],
        out_weight,
        ends,
        query_gain[None],
        key_gain[None],
    )
    dk_back, dv_back, shard = pl.pallas_call(
        functools.partial(exchange_kernel, n, side),
        out_shape=(
            struct((tokens, inner), BF16),
            struct((tokens, inner), BF16),
            struct((width, model // (2 * chips)), F32),
        ),
        in_specs=[anywhere] * 3,
        out_specs=(anywhere, anywhere, vmem),
        scratch_shapes=[
            pltpu.VMEM((width // 2, model), BF16),
            pltpu.VMEM((width // 2, model), BF16),
            pltpu.VMEM((chips, width // 2, model // chips), BF16),
            pltpu.VMEM((chips, width // 2, model // chips), BF16),
            pltpu.VMEM((width // 2, model // chips), F32),
            pltpu.VMEM((width // 2, 256), F32),
            dma((2, n)),
            dma((2, n)),
            dma((2,)),
            dma((2,)),
            dma((chips,)),
            dma((chips,)),
            dma((3,)),
        ],
        compiler_params=pltpu.CompilerParams(
            collective_id=2, has_side_effects=True, vmem_limit_bytes=60 * 1024 * 1024
        ),
        name="exchange",
    )(dk, dv, wp)
    weight_grad, gains, norm = pl.pallas_call(
        functools.partial(norm_kernel, n, side),
        out_shape=(
            struct(shard.shape, F32),
            struct((8, HEAD_DIM), F32),
            struct((8, 128), F32),
        ),
        in_specs=[vmem, vmem],
        out_specs=(vmem, vmem, vmem),
        scratch_shapes=[
            pltpu.VMEM((n, 8, 128), F32),
            pltpu.VMEM((2 * chips, 8, 128), F32),
            dma((n,)),
            dma((n,)),
            dma((2 * chips,)),
            dma((2 * chips,)),
        ],
        compiler_params=pltpu.CompilerParams(collective_id=3, has_side_effects=True),
        name="norm",
    )(shard, gain)
    return (
        dq[None],
        dk_back[None],
        dv_back[None],
        weight_grad,
        gains[0],
        gains[1],
        norm[0, 0],
    )


def solution(mesh):
    n = mesh.shape["seq"]
    torus = Mesh(mesh.devices.reshape(4, 4, 2, n), ("dp_0", "dp_1", "dp_2", "seq"))
    return jax.shard_map(
        functools.partial(local, n, 4),
        mesh=torus,
        in_specs=(
            P(DP, "seq", None),
            P(DP, "seq", None),
            P(DP, "seq", None),
            P(DP, "seq", None),
            P(DP, None),
            P("seq", None),
            P(),
            P(),
        ),
        out_specs=(
            P(DP, "seq", None),
            P(DP, "seq", None),
            P(DP, "seq", None),
            P("seq", DP),
            P(),
            P(),
            P(),
        ),
        check_vma=False,
    )
```

time: 432 us -> 283 us (0.66)
  Pallas kernels: 0 us -> 273 us
  waiting for transfers between devices: 164 us -> 0 us
  matrix products: 86.5 us -> 0 us
  local copies, waits for them, and re-layouts: 60.2 us -> 8.14 us
  blocking collectives: 40.9 us -> 0 us
  starting transfers between devices: 29.1 us -> 0 us
  other arithmetic: 26.9 us -> 1.33 us
  between operations: 17.6 us -> 0.68 us
    pallas_call x0 -> x3, Pallas kernels: none -> 273 us  [the longest x1 204 us: local(): pl.pallas_call(functools.partial(attention_kernel, n), out_shape=(struct(...]
    all_to_all x6 -> x0, waiting for transfers between devices: 129 us -> none  [the longest x1 30.4 us: local(): lax.all_to_all(key_rows[0], 'seq', split_axis=1, concat_axis=0, tiled=True)]
    dot_general x14 -> x0, matrix products: 86.5 us -> none  [the longest x2 20.7 us: backward_block(): jnp.einsum('hqk,qhd->khd', d_scores, query_block, preferred_element_type=...]
    psum x4 -> x0, blocking collectives: 40.9 us -> none  [one_axis_at_a_time(): array = lax.psum(array, axis)]
    all_gather x1 -> x0, waiting for transfers between devices: 34.3 us -> none  [local(): out_full = lax.all_gather(out_grad[0], 'seq', axis=0, tiled=True)]
    all_to_all x6 -> x0, starting transfers between devices: 29 us -> none  [the longest x1 9 us: local(): lax.all_to_all(query_rows[0], 'seq', split_axis=1, concat_axis=0, tiled=T...]
    while x25 -> x0, local copies, waits for them, and re-layouts: 18.8 us -> none  [the longest x3 7.67 us: local(): lax.map(forward_block, jnp.arange(blocks, dtype=jnp.int32))]
    reduce_sum x8 -> x0, other arithmetic: 11 us -> none  [the longest x2 4.63 us: norm_back(): gain_part = jnp.sum(unit * d_norm, axis=(0, 1))]
  transfers between devices with their start and end apart: 8 -> 0, of which waited for: 7 -> 0; matrix products, arithmetic and copies ran while one was open for 35% -> 0% of each run, Pallas kernels for 0% -> 0%
where the time goes in v1:
time: 283 us
  Pallas kernels  273 us (96%)
  local copies, waits for them, and re-layouts  8.14 us (3%)
    pallas_call x1, Pallas kernels, local(): pl.pallas_call(functools.partial(attention_kernel, n), out_shape=(struct(...  204 us
    pallas_call x1, Pallas kernels, local(): pl.pallas_call(functools.partial(exchange_kernel, n, side), out_shape=(st...  51.5 us
    pallas_call x1, Pallas kernels, local(): pl.pallas_call(functools.partial(norm_kernel, n, side), out_shape=(struct...  16.9 us
    unnamed x8, local copies, waits for them, and re-layouts  5.69 us

profile of v1, /device:TPU:1, one launch (start us, length us, event | category | flops | bytes accessed | tf_op | source)
XLA Modules:
  0.0 282.9 jit_solution(15015301920576218602)
XLA Ops:
  0.6 1.3 reduce-window.9
  2.0 204.3 %attention.1 = (bf16[128,3072]{1,0:T(8,128)(2,1)}, bf16[1024,384]{1,0:T(8,128)(2,1)}, bf16[1024,384]{1,0:T(8,128)(2,1)}, bf16[384,6144]{1,0:T(8,128)(2,1)}, f32[8,128]{1,0:T(8,128)}) custom-call(bf16[128,3072]{1,0:T(8,128)(2,1)} %bitcast.17, bf16[128,3072]{1,0:T(8,128)(2,1)} %bitcast.18, bf16[128,3072]{1,0:T(8,128)(2,1)} %bitcast.19, ...), custom_call_target="tpu_custom_call" | custom-call | tf_op jit(solution)/shard_map/attention/pallas_call | solution.py:572
  206.3 0.0 copy-start
  206.3 51.5 %exchange.1 = (bf16[128,3072]{1,0:T(8,128)(2,1)}, bf16[128,3072]{1,0:T(8,128)(2,1)}, f32[384,192]{1,0:T(8,128)}) custom-call(bf16[1024,384]{1,0:T(8,128)(2,1)} %get-tuple-element.19.dk_ref, bf16[1024,384]{1,0:T(8,128)(2,1)} %get-tuple-element.20.dv_ref, bf16[384,6144]{1,0:T(8,128)(2,1)} %get-tuple-element.21.wp_ref), custom_call_target="tpu_custom_call" | custom-call | tf_op jit(solution)/shard_map/exchange/pallas_call | solution.py:618
  257.8 0.0 copy-start.1
  257.8 16.9 %norm.1 = (f32[384,192]{1,0:T(8,128)}, f32[8,128]{1,0:T(8,128)}, f32[8,128]{1,0:T(8,128)}) custom-call(f32[384,192]{1,0:T(8,128)} %get-tuple-element.24.shard_ref, f32[8,128]{1,0:T(8,128)} %get-tuple-element.25.gain_ref), custom_call_target="tpu_custom_call" | custom-call | tf_op jit(solution)/shard_map/norm/pallas_call | solution.py:647
  274.8 1.2 slice.11
  276.0 1.9 copy.15
  277.8 1.3 slice_bitcast_fusion
  279.1 0.0 copy-done
  279.1 0.9 copy.19
  280.0 2.1 copy.20
  282.0 0.0 copy-done.1
  282.0 0.9 copy.21
Async XLA Ops:
  206.3 72.8 %copy-start = (bf16[128,3072]{1,0:T(8,128)(2,1)S(1)}, bf16[128,3072]{1,0:T(8,128)(2,1)}, u32[]{:S(2)}) copy-start(bf16[128,3072]{1,0:T(8,128)(2,1)} %get-tuple-element.18) | copy-start | bytes 2359300
  257.8 24.2 %copy-start.1 = (bf16[128,3072]{1,0:T(8,128)(2,1)S(1)}, bf16[128,3072]{1,0:T(8,128)(2,1)}, u32[]{:S(2)}) copy-start(bf16[128,3072]{1,0:T(8,128)(2,1)} %get-tuple-element.23) | copy-start | bytes 2359300

commit v2 on v0

v2 whole, which is shorter than its diff:
```python
import functools

import jax
import jax.numpy as jnp
from jax import lax
from jax.experimental import pallas as pl
from jax.experimental.pallas import tpu as pltpu
from jax.sharding import Mesh
from jax.sharding import PartitionSpec as P

HEAD_DIM = 128
MAX_NORM = 768
EPS = 1e-06
DP = ("dp_0", "dp_1", "dp_2")
MESH = pl.DeviceIdType.MESH
F32 = jnp.float32
BF16 = jnp.bfloat16
NN = (((1,), (0,)), ((), ()))
NT = (((1,), (1,)), ((), ()))
SUBS = 4


def dot(a, b, dims=NN):
    return lax.dot_general(a, b, dims, preferred_element_type=F32)


def seg_of(places, lengths_ref):
    seg = jnp.zeros(places.shape, jnp.int32)
    end = jnp.int32(0)
    for c in range(lengths_ref.shape[0]):
        end = end + lengths_ref[c]
        seg = seg + (places >= end).astype(jnp.int32)
    return seg


def kernel(
    n,
    side,
    q_hbm,
    k_hbm,
    v_hbm,
    do_hbm,
    w_hbm,
    lengths_ref,
    qg_ref,
    kg_ref,
    dq_out,
    dk_out,
    dv_out,
    w_out,
    qgain_out,
    kgain_out,
    norm_out,
    qkv,
    kn,
    knt,
    vt,
    do_all,
    w,
    wacc,
    dkt,
    dvt,
    datt,
    attnt,
    probs,
    dqs,
    dkv,
    gain,
    wpb,
    theirs,
    packed,
    slots,
    reduced,
    final,
    z_slots,
    dp_slots,
    qkv_send,
    qkv_recv,
    ag_send,
    ag_recv,
    dq_send,
    dq_recv,
    dkv_send,
    dkv_recv,
    swap_send,
    swap_recv,
    x_send,
    x_recv,
    last_send,
    last_recv,
    z_send,
    z_recv,
    dp_send,
    dp_recv,
    own_sem,
):
    me = lax.axis_index("seq")
    y, x, core = (lax.axis_index(name) for name in DP)
    other = 1 - core
    sign = 1 - 2 * core
    tokens = q_hbm.shape[0]
    total = tokens * n
    width = q_hbm.shape[1] // n
    heads = width // HEAD_DIM
    model = do_hbm.shape[1]
    quarter = model // SUBS
    scale = HEAD_DIM ** (-0.5)
    up = lax.rem(me + sign + n, n)
    down = lax.rem(me - sign + n, n)
    a_steps = n // 2
    b_steps = n - 1 - a_steps
    chips = side * side
    chunk = model // chips
    per_sub = chips // SUBS
    half = width // 2
    here = y * side + x
    group = 2 * chips
    in_group = here * 2 + core

    def columns(index):
        return pl.ds(pl.multiple_of(index * width, width), width)

    def rows_of(index):
        return pl.ds(pl.multiple_of(index * tokens, tokens), tokens)

    def half_of(index):
        return pl.ds(pl.multiple_of(index * half, half), half)

    def sub_of(index):
        return pl.ds(index * quarter, quarter)

    def peer(d):
        return lax.rem(me + d, n)

    def z_peer(d):
        return {"seq": peer(d)}, peer(d)

    def chip(d):
        place = lax.rem(here + d, chips)
        return {"dp_0": place // side, "dp_1": lax.rem(place, side)}, place

    def dp_peer(d):
        place = lax.rem(in_group + d, group)
        return {
            "dp_0": place // (2 * side),
            "dp_1": lax.rem(place // 2, side),
            "dp_2": lax.rem(place, 2),
        }, place

    def remote(src, dst, send, recv, to):
        return pltpu.make_async_remote_copy(
            src_ref=src, dst_ref=dst, send_sem=send, recv_sem=recv, device_id=to, device_id_type=MESH
        )

    barrier = pltpu.get_barrier_semaphore()
    for d in range(1, n):
        pl.semaphore_signal(barrier, inc=1, device_id=z_peer(d)[0], device_id_type=MESH)
    for d in range(1, group):
        pl.semaphore_signal(barrier, inc=1, device_id=dp_peer(d)[0], device_id_type=MESH)

    own_copies = [
        pltpu.make_async_copy(ref.at[:, columns(me)], qkv.at[i, rows_of(me)], own_sem.at[i])
        for i, ref in enumerate((q_hbm, k_hbm, v_hbm))
    ]
    do_copies = [
        pltpu.make_async_copy(do_hbm.at[:, sub_of(sub)], do_all.at[me, sub], own_sem.at[4 + sub])
        for sub in range(SUBS)
    ]
    w_copy = pltpu.make_async_copy(w_hbm, w, own_sem.at[3])
    for copy in own_copies + do_copies + [w_copy]:
        copy.start()
    pl.semaphore_wait(barrier, n + group - 2)

    order = [4, 3, 5, 2, 6, 1, 7] if n == 8 else list(range(1, n))
    arrays = ((1, k_hbm), (2, v_hbm), (0, q_hbm))

    def qkv_copy(i, ref, d, place):
        to = peer(d)
        return remote(
            ref.at[:, columns(to)],
            qkv.at[i, rows_of(place)],
            qkv_send.at[i, d],
            qkv_recv.at[i, place],
            {"seq": to},
        )

    for i, ref in arrays:
        for d in order:
            qkv_copy(i, ref, d, me).start()

    def ring(direction, step, sub, block, to, own=False):
        return remote(
            do_hbm.at[:, sub_of(sub)] if own else do_all.at[block, sub],
            do_all.at[block, sub],
            ag_send.at[direction, step, sub],
            ag_recv.at[block, sub],
            {"seq": to},
        )

    for sub in range(SUBS):
        ring(0, 0, sub, me, up, True).start()
        ring(1, 0, sub, me, down, True).start()

    dkt[...] = jnp.zeros(dkt.shape, F32)
    dvt[...] = jnp.zeros(dvt.shape, F32)
    gain[...] = jnp.zeros(gain.shape, F32)

    def clear(i, carry):
        wacc[:, pl.ds(pl.multiple_of(i * 512, 512), 512)] = jnp.zeros((width, 512), F32)
        return carry

    lax.fori_loop(0, model // 512, clear, 0)
    kg = kg_ref[...]
    qg = qg_ref[...]
    seg_k = seg_of(lax.broadcasted_iota(jnp.int32, (1, total), 1), lengths_ref)

    for copy in own_copies:
        copy.wait()
    for i, ref in arrays:
        for d in range(1, n):
            qkv_copy(i, ref, d, peer(d)).wait_recv()

    def norm_rows(i, rows, cols):
        block = qkv[i, rows, cols].astype(F32)
        inverse = lax.rsqrt(jnp.mean(block * block, axis=-1, keepdims=True) + EPS)
        return block * inverse, inverse

    def norm_back(unit, inverse, weight, d_normed):
        d_unit = d_normed * weight
        d_rows = inverse * (d_unit - unit * jnp.mean(unit * d_unit, axis=-1, keepdims=True))
        return d_rows.astype(BF16)

    for h in range(heads):
        cols = pl.ds(h * HEAD_DIM, HEAD_DIM)

        def prepare(j, carry, cols=cols):
            rows = pl.ds(pl.multiple_of(j * 256, 256), 256)
            normed = norm_rows(1, rows, cols)[0] * kg
            kn[rows, cols] = normed.astype(BF16)
            knt[cols, rows] = jnp.transpose(normed).astype(BF16)
            vt[cols, rows] = jnp.transpose(qkv[2, rows, cols].astype(F32)).astype(BF16)
            return carry

        lax.fori_loop(0, total // 256, prepare, 0)

    def forward(j, carry):
        rows = pl.ds(pl.multiple_of(j * 256, 256), 256)
        places = lax.broadcasted_iota(jnp.int32, (256, 1), 0) + j * 256
        same = seg_of(places, lengths_ref) == seg_k
        for h in range(heads):
            cols = pl.ds(h * HEAD_DIM, HEAD_DIM)
            qn = (norm_rows(0, rows, cols)[0] * qg).astype(BF16)
            expo = jnp.where(same, jnp.exp(dot(qn, knt[cols, :]) * scale), 0.0)
            prob = (expo * (1.0 / jnp.sum(expo, axis=-1, keepdims=True))).astype(BF16)
            probs[h, rows, :] = prob
            attn = dot(prob, qkv[2, :, cols])
            attnt[cols, rows] = jnp.transpose(attn).astype(BF16)
        return carry

    lax.fori_loop(0, total // 256, forward, 0)
    for copy in do_copies:
        copy.wait()
    w_copy.wait()

    def project(t, sub):
        part = sub_of(sub)
        datt[...] += dot(do_all[t, sub], w[:, part], NT)

    def weigh(t, sub):
        def piece(j, c):
            part = pl.ds(pl.multiple_of(j * 512, 512), 512)
            into = pl.ds(pl.multiple_of(sub * quarter + j * 512, 512), 512)
            wacc[:, into] += dot(attnt[:, rows_of(t)], do_all[t, sub, :, part])
            return c

        lax.fori_loop(0, quarter // 512, piece, 0)

    def backward(t, h):
        rows = rows_of(t)
        cols = pl.ds(h * HEAD_DIM, HEAD_DIM)
        unit, inverse = norm_rows(0, rows, cols)
        normed = unit * qg
        dattn = datt[:, cols]
        prob = probs[h, rows, :]
        prob32 = prob.astype(F32)
        d_probs = dot(dattn.astype(BF16), vt[cols, :])
        row_sum = jnp.sum(prob32 * d_probs, axis=-1, keepdims=True)
        d_scores = (prob32 * (d_probs - row_sum) * scale).astype(BF16)
        dvt[cols, :] += dot(jnp.transpose(dattn).astype(BF16), prob)
        dkt[cols, :] += dot(jnp.transpose(normed).astype(BF16), d_scores)
        d_normed = dot(d_scores, kn[:, cols])
        gain[0:1, :] += jnp.sum(unit * d_normed, axis=0, keepdims=True)
        dqs[t, :, cols] = norm_back(unit, inverse, qg, d_normed)

    def dq_copy(t, place):
        return remote(
            dqs.at[t], dq_out.at[:, columns(place)], dq_send.at[t], dq_recv.at[place], {"seq": t}
        )

    def body(i, carry):
        step = (i + 1) // 2
        odd = lax.rem(i, 2)
        shift = sign * step
        t = lax.rem(me + shift - 2 * odd * shift + n, n)
        a_block = lax.rem(me - shift + n, n)
        b_block = lax.rem(me + shift + n, n)

        @pl.when(odd == 1)
        def _():
            for sub in range(SUBS):
                ring(0, step - 1, sub, a_block, up).wait_recv()
                ring(0, step, sub, a_block, up).start()
            for sub in range(SUBS):
                ring(1, step - 1, sub, b_block, down).wait_recv()

                @pl.when(step < b_steps)
                def _():
                    ring(1, step, sub, b_block, down).start()

        datt[...] = jnp.zeros(datt.shape, F32)
        for sub in range(SUBS):
            project(t, sub)
        for h in range(heads):
            backward(t, h)

        @pl.when(i > 0)
        def _():
            dq_copy(t, me).start()

        for sub in range(SUBS):
            weigh(t, sub)
        return carry

    lax.fori_loop(0, n - 1, body, 0)

    own_dq = pltpu.make_async_copy(dqs.at[me], dq_out.at[:, columns(me)], own_sem.at[0])
    own_dq.start()

    t = lax.rem(me - sign * a_steps + n, n)
    datt[...] = jnp.zeros(datt.shape, F32)

    def swap(sub):
        part = sub_of(sub)
        return remote(
            wpb.at[half_of(other), part],
            theirs.at[:, part],
            swap_send.at[sub],
            swap_recv.at[sub],
            {"dp_2": other},
        )

    def scatter(d, place_here):
        target, place = chip(d)
        return remote(
            packed.at[place], slots.at[place_here], x_send.at[place], x_recv.at[place_here], target
        )

    def merge(sub):
        swap(sub).wait_recv()

        def piece(j, carry):
            part = pl.ds(pl.multiple_of(j * chunk, chunk), chunk)
            packed[j] = (wpb[half_of(core), part].astype(F32) + theirs[:, part].astype(F32)).astype(BF16)
            return carry

        lax.fori_loop(sub * per_sub, (sub + 1) * per_sub, piece, 0)

    def scatter_of(place):
        return remote(
            packed.at[place],
            slots.at[here],
            x_send.at[place],
            x_recv.at[here],
            {"dp_0": place // side, "dp_1": lax.rem(place, side)},
        )

    def send_sub(sub):
        def one(j, carry):
            place = sub * per_sub + lax.rem(here + j, per_sub)

            @pl.when(place != here)
            def _():
                scatter_of(place).start()

            return carry

        lax.fori_loop(0, per_sub, one, 0)

    for sub in range(SUBS):
        ring(0, a_steps - 1, sub, t, up).wait_recv()
        weigh(t, sub)

        def narrow(j, carry, sub=sub):
            part = pl.ds(pl.multiple_of(sub * quarter + j * 512, 512), 512)
            wpb[:, part] = wacc[:, part].astype(BF16)
            return carry

        lax.fori_loop(0, quarter // 512, narrow, 0)
        if sub > 0:
            merge(sub - 1)
        project(t, sub)
        swap(sub).start()
        if sub > 0:
            send_sub(sub - 1)

    def dkv_copy(i, h, d, place):
        to = peer(d)
        return remote(
            dkv.at[i, rows_of(to), pl.ds(h * HEAD_DIM, HEAD_DIM)],
            (dk_out, dv_out)[i].at[:, pl.ds(pl.multiple_of(place * width + h * HEAD_DIM, HEAD_DIM), HEAD_DIM)],
            dkv_send.at[i, h, d],
            dkv_recv.at[i, h, place],
            {"seq": to},
        )

    for h in range(heads):
        cols = pl.ds(h * HEAD_DIM, HEAD_DIM)
        backward(t, h)

        def finish(j, carry, cols=cols):
            rows = pl.ds(pl.multiple_of(j * 256, 256), 256)
            dkv[1, rows, cols] = jnp.transpose(dvt[cols, rows]).astype(BF16)
            unit, inverse = norm_rows(1, rows, cols)
            d_normed = jnp.transpose(dkt[cols, rows])
            gain[1:2, :] += jnp.sum(unit * d_normed, axis=0, keepdims=True)
            dkv[0, rows, cols] = norm_back(unit, inverse, kg, d_normed)
            return carry

        lax.fori_loop(0, total // 256, finish, 0)
        for i in (1, 0):
            for d in order:
                dkv_copy(i, h, d, me).start()
        if h == 0:
            merge(SUBS - 1)
            send_sub(SUBS - 1)
    dq_copy(t, me).start()
    own_dkv = [
        pltpu.make_async_copy(dkv.at[i, rows_of(me)], out.at[:, columns(me)], own_sem.at[1 + i])
        for i, out in enumerate((dk_out, dv_out))
    ]
    for copy in own_dkv:
        copy.start()

    reduced[...] = packed[here].astype(F32)
    for d in range(1, chips):
        place = chip(d)[1]
        scatter(d, place).wait_recv()
        reduced[...] += slots[place].astype(F32)

    def window(index):
        return pl.ds(pl.multiple_of(index * 128, 128), 256)

    shard_width = chunk // 2
    last = remote(reduced.at[:, window(other)], final, last_send.at[0], last_recv.at[0], {"dp_2": other})
    last.start()

    def pick(block):
        return jnp.where(core == 0, block[:, :shard_width], block[:, 256 - shard_width :])

    mine = pick(reduced[:, window(core)])
    w_out[half_of(core), :] = mine
    square = jnp.sum(mine * mine)
    row = lax.broadcasted_iota(jnp.int32, (8, 128), 0)
    last.wait_recv()
    rest = pick(final[...])
    w_out[half_of(other), :] = rest
    square = square + jnp.sum(rest * rest)
    z_slots[me] = jnp.where(row == 2, square, gain[...])

    def spread(buffer, peers, count, sends, recvs, place):
        def copy(d, source):
            return remote(buffer.at[source], buffer.at[source], sends.at[d], recvs.at[source], peers(d)[0])

        for d in range(1, count):
            copy(d, place).start()
        for d in range(1, count):
            copy(d, peers(d)[1]).wait_recv()
        result = buffer[0]
        for index in range(1, count):
            result = result + buffer[index]
        for d in range(1, count):
            copy(d, place).wait_send()
        return result

    dp_slots[in_group] = spread(z_slots, z_peer, n, z_send, z_recv, me)
    summed = spread(dp_slots, dp_peer, group, dp_send, dp_recv, in_group)
    gains = jnp.where(row < 2, summed, 0.0)
    squares = summed[2:3, 0:1] + jnp.sum(gains * gains)
    norm = jnp.sqrt(squares)
    factor = jnp.minimum(1.0, MAX_NORM / (norm + EPS))
    qgain_out[...] = gains[0:1] * factor
    kgain_out[...] = gains[1:2] * factor
    norm_out[...] = norm
    w_out[...] = w_out[...] * factor

    last.wait_send()
    own_dq.wait()
    for copy in own_dkv:
        copy.wait()
    for i, ref in arrays:
        for d in order:
            qkv_copy(i, ref, d, me).wait_send()
    for sub in range(SUBS):
        swap(sub).wait_send()
        for step in range(a_steps):
            ring(0, step, sub, me, up).wait_send()
        for step in range(b_steps):
            ring(1, step, sub, me, down).wait_send()
    for d in range(1, chips):
        scatter(d, here).wait_send()
    for d in range(1, n):
        dq_copy(peer(d), me).wait_send()
        dq_copy(peer(d), peer(d)).wait_recv()
        for i in (0, 1):
            for h in range(heads):
                dkv_copy(i, h, d, me).wait_send()
                dkv_copy(i, h, d, peer(d)).wait_recv()


def local(n, side, query_rows, key_rows, value_rows, out_grad, clip_lengths, out_weight, query_gain, key_gain):
    tokens, inner = query_rows.shape[1:]
    model = out_grad.shape[2]
    width = inner // n
    heads = width // HEAD_DIM
    total = tokens * n
    vmem = pl.BlockSpec(memory_space=pltpu.VMEM)
    smem = pl.BlockSpec(memory_space=pltpu.SMEM)
    anywhere = pl.BlockSpec(memory_space=pl.ANY)
    dma = pltpu.SemaphoreType.DMA
    struct = jax.ShapeDtypeStruct
    chips = side * side
    chunk = model // chips
    dq, dk, dv, weight_grad, qgain, kgain, norm = pl.pallas_call(
        functools.partial(kernel, n, side),
        out_shape=(
            struct((tokens, inner), BF16),
            struct((tokens, inner), BF16),
            struct((tokens, inner), BF16),
            struct((width, chunk // 2), F32),
            struct((1, HEAD_DIM), F32),
            struct((1, HEAD_DIM), F32),
            struct((1, 1), F32),
        ),
        in_specs=[anywhere] * 5 + [smem, vmem, vmem],
        out_specs=(anywhere, anywhere, anywhere, vmem, vmem, vmem, vmem),
        scratch_shapes=[
            pltpu.VMEM((3, total, width), BF16),
            pltpu.VMEM((total, width), BF16),
            pltpu.VMEM((width, total), BF16),
            pltpu.VMEM((width, total), BF16),
            pltpu.VMEM((n, SUBS, tokens, model // SUBS), BF16),
            pltpu.VMEM((width, model), BF16),
            pltpu.VMEM((width, model), F32),
            pltpu.VMEM((width, total), F32),
            pltpu.VMEM((width, total), F32),
            pltpu.VMEM((tokens, width), F32),
            pltpu.VMEM((width, total), BF16),
            pltpu.VMEM((heads, total, total), BF16),
            pltpu.VMEM((n, tokens, width), BF16),
            pltpu.VMEM((2, total, width), BF16),
            pltpu.VMEM((8, HEAD_DIM), F32),
            pltpu.VMEM((width, model), BF16),
            pltpu.VMEM((width // 2, model), BF16),
            pltpu.VMEM((chips, width // 2, chunk), BF16),
            pltpu.VMEM((chips, width // 2, chunk), BF16),
            pltpu.VMEM((width // 2, chunk), F32),
            pltpu.VMEM((width // 2, 256), F32),
            pltpu.VMEM((n, 8, 128), F32),
            pltpu.VMEM((2 * chips, 8, 128), F32),
            dma((3, n)),
            dma((3, n)),
            dma((2, n // 2, SUBS)),
            dma((n, SUBS)),
            dma((n,)),
            dma((n,)),
            dma((2, heads, n)),
            dma((2, heads, n)),
            dma((SUBS,)),
            dma((SUBS,)),
            dma((chips,)),
            dma((chips,)),
            dma((1,)),
            dma((1,)),
            dma((n,)),
            dma((n,)),
            dma((2 * chips,)),
            dma((2 * chips,)),
            dma((8,)),
        ],
        compiler_params=pltpu.CompilerParams(
            collective_id=1, has_side_effects=True, vmem_limit_bytes=67043328
        ),
        name="fused",
    )(
        query_rows[0],
        key_rows[0],
        value_rows[0],
        out_grad[0],
        out_weight,
        clip_lengths[0],
        query_gain[None],
        key_gain[None],
    )
    return (
        dq[None],
        dk[None],
        dv[None],
        weight_grad,
        qgain.reshape(HEAD_DIM),
        kgain.reshape(HEAD_DIM),
        norm.reshape(()),
    )


def solution(mesh):
    n = mesh.shape["seq"]
    torus = Mesh(mesh.devices.reshape(4, 4, 2, n), ("dp_0", "dp_1", "dp_2", "seq"))
    return jax.shard_map(
        functools.partial(local, n, 4),
        mesh=torus,
        in_specs=(
            P(DP, "seq", None),
            P(DP, "seq", None),
            P(DP, "seq", None),
            P(DP, "seq", None),
            P(DP, None),
            P("seq", None),
            P(),
            P(),
        ),
        out_specs=(
            P(DP, "seq", None),
            P(DP, "seq", None),
            P(DP, "seq", None),
            P("seq", DP),
            P(),
            P(),
            P(),
        ),
        check_vma=False,
    )
```

time: 432 us -> 265 us (0.61)
  Pallas kernels: 0 us -> 253 us
  waiting for transfers between devices: 164 us -> 0 us
  matrix products: 86.5 us -> 0 us
  local copies, waits for them, and re-layouts: 60.2 us -> 9.08 us
  blocking collectives: 40.9 us -> 0 us
  starting transfers between devices: 29.1 us -> 0 us
  other arithmetic: 26.9 us -> 0 us
  between operations: 17.6 us -> 2.36 us
    pallas_call x0 -> x1, Pallas kernels: none -> 253 us  [local(): pl.pallas_call(functools.partial(kernel, n, side), out_shape=(struct((tok...]
    all_to_all x6 -> x0, waiting for transfers between devices: 129 us -> none  [the longest x1 30.4 us: local(): lax.all_to_all(key_rows[0], 'seq', split_axis=1, concat_axis=0, tiled=True)]
    dot_general x14 -> x0, matrix products: 86.5 us -> none  [the longest x2 20.7 us: backward_block(): jnp.einsum('hqk,qhd->khd', d_scores, query_block, preferred_element_type=...]
    psum x4 -> x0, blocking collectives: 40.9 us -> none  [one_axis_at_a_time(): array = lax.psum(array, axis)]
    all_gather x1 -> x0, waiting for transfers between devices: 34.3 us -> none  [local(): out_full = lax.all_gather(out_grad[0], 'seq', axis=0, tiled=True)]
    all_to_all x6 -> x0, starting transfers between devices: 29 us -> none  [the longest x1 9 us: local(): lax.all_to_all(query_rows[0], 'seq', split_axis=1, concat_axis=0, tiled=T...]
    while x25 -> x0, local copies, waits for them, and re-layouts: 18.8 us -> none  [the longest x3 7.67 us: local(): lax.map(forward_block, jnp.arange(blocks, dtype=jnp.int32))]
    reduce_sum x8 -> x0, other arithmetic: 11 us -> none  [the longest x2 4.63 us: norm_back(): gain_part = jnp.sum(unit * d_norm, axis=(0, 1))]
  transfers between devices with their start and end apart: 8 -> 0, of which waited for: 7 -> 0; matrix products, arithmetic and copies ran while one was open for 35% -> 0% of each run, Pallas kernels for 0% -> 0%
where the time goes in v2:
time: 265 us
  Pallas kernels  253 us (95%)
  local copies, waits for them, and re-layouts  9.08 us (3%)
    pallas_call x1, Pallas kernels, local(): pl.pallas_call(functools.partial(kernel, n, side), out_shape=(struct((tok...  253 us
    unnamed x10, local copies, waits for them, and re-layouts  9.08 us

profile of v2, /device:TPU:1, one launch (start us, length us, event | category | flops | bytes accessed | tf_op | source)
XLA Modules:
  0.0 264.7 jit_solution(12280622394219332526)
XLA Ops:
  0.6 253.3 %fused.1 = (bf16[128,3072]{1,0:T(8,128)(2,1)}, bf16[128,3072]{1,0:T(8,128)(2,1)}, bf16[128,3072]{1,0:T(8,128)(2,1)}, f32[384,192]{1,0:T(8,128)}, f32[1,128]{1,0:...) custom-call(bf16[128,3072]{1,0:T(8,128)(2,1)} %bitcast.14, bf16[128,3072]{1,0:T(8,128)(2,1)} %bitcast.15, ...), custom_call_target="tpu_custom_call" | custom-call | tf_op jit(solution)/shard_map/fused/pallas_call | solution.py:533
  253.9 0.0 copy-start.1
  253.9 0.0 copy-start
  253.9 1.9 copy.15
  255.8 2.1 copy.22
  257.9 2.1 copy.23
  259.9 2.1 copy.24
  262.0 0.0 copy-done.1
  262.0 0.5 copy.25
  262.5 0.0 copy-done
  262.5 0.5 copy.26
Async XLA Ops:
  253.9 8.1 %copy-start.1 = (f32[1,128]{1,0:T(1,128)S(1)}, f32[1,128]{1,0:T(1,128)}, u32[]{:S(2)}) copy-start(f32[1,128]{1,0:T(1,128)} %get-tuple-element.18) | copy-start | bytes 1540
  253.9 8.6 %copy-start = (f32[1,128]{1,0:T(1,128)S(1)}, f32[1,128]{1,0:T(1,128)}, u32[]{:S(2)}) copy-start(f32[1,128]{1,0:T(1,128)} %get-tuple-element.19) | copy-start | bytes 1540

commit v3 on v2

--- a/solution.py
+++ b/solution.py
@@ -310,7 +310,6 @@
             for sub in range(SUBS):
                 ring(0, step - 1, sub, a_block, up).wait_recv()
                 ring(0, step, sub, a_block, up).start()
-            for sub in range(SUBS):
                 ring(1, step - 1, sub, b_block, down).wait_recv()
 
                 @pl.when(step < b_steps)
@@ -323,16 +322,23 @@
         for h in range(heads):
             backward(t, h)
 
-        @pl.when(i > 0)
-        def _():
-            dq_copy(t, me).start()
-
         for sub in range(SUBS):
             weigh(t, sub)
+
+        @pl.when(i == 2 * b_steps - 1)
+        def _():
+            def early(j, c):
+                dq_copy(lax.rem(me + sign * (j - b_steps) + n, n), me).start()
+                return c
+
+            lax.fori_loop(0, b_steps, early, 0)
+            lax.fori_loop(b_steps + 1, 2 * b_steps, early, 0)
+
         return carry
 
     lax.fori_loop(0, n - 1, body, 0)
 
+    dq_copy(lax.rem(me + sign * b_steps + n, n), me).start()
     own_dq = pltpu.make_async_copy(dqs.at[me], dq_out.at[:, columns(me)], own_sem.at[0])
     own_dq.start()
 
@@ -465,7 +471,7 @@
     rest = pick(final[...])
     w_out[half_of(other), :] = rest
     square = square + jnp.sum(rest * rest)
-    z_slots[me] = jnp.where(row == 2, square, gain[...])
+    dp_slots[in_group] = jnp.where(row == 2, square, gain[...])
 
     def spread(buffer, peers, count, sends, recvs, place):
         def copy(d, source):
@@ -482,8 +488,8 @@
             copy(d, place).wait_send()
         return result
 
-    dp_slots[in_group] = spread(z_slots, z_peer, n, z_send, z_recv, me)
-    summed = spread(dp_slots, dp_peer, group, dp_send, dp_recv, in_group)
+    z_slots[me] = spread(dp_slots, dp_peer, group, dp_send, dp_recv, in_group)
+    summed = spread(z_slots, z_peer, n, z_send, z_recv, me)
     gains = jnp.where(row < 2, summed, 0.0)
     squares = summed[2:3, 0:1] + jnp.sum(gains * gains)
     norm = jnp.sqrt(squares)
@@ -515,6 +521,31 @@
             for h in range(heads):
                 dkv_copy(i, h, d, me).wait_send()
                 dkv_copy(i, h, d, peer(d)).wait_recv()
+
+
+def write_kernel(dq_in, dk_in, dv_in, w_in, qgain_in, kgain_in, norm_in, dq_out, dk_out, dv_out, w_out, qgain_out, kgain_out, norm_out, held, in_sem, out_sem):
+    pieces = held.shape[1]
+    rows = held.shape[2]
+    refs = ((dq_in, dq_out), (dk_in, dk_out), (dv_in, dv_out))
+
+    def load(i, p):
+        return pltpu.make_async_copy(refs[i][0].at[pl.ds(p * rows, rows)], held.at[i, p], in_sem.at[i, p])
+
+    def store(i, p):
+        return pltpu.make_async_copy(held.at[i, p], refs[i][1].at[pl.ds(p * rows, rows)], out_sem.at[i, p])
+
+    every = [(i, p) for i in range(3) for p in range(pieces)]
+    for i, p in every:
+        load(i, p).start()
+    w_out[...] = jnp.transpose(w_in[...])
+    qgain_out[...] = qgain_in[...]
+    kgain_out[...] = kgain_in[...]
+    norm_out[...] = norm_in[...]
+    for i, p in every:
+        load(i, p).wait()
+        store(i, p).start()
+    for i, p in every:
+        store(i, p).wait()
 
 
 def local(n, side, query_rows, key_rows, value_rows, out_grad, clip_lengths, out_weight, query_gain, key_gain):
@@ -601,11 +632,21 @@
         query_gain[None],
         key_gain[None],
     )
+    rows = struct((tokens, inner), BF16)
+    gain = struct((1, HEAD_DIM), F32)
+    dq, dk, dv, weight_grad, qgain, kgain, norm = pl.pallas_call(
+        write_kernel,
+        out_shape=(rows, rows, rows, struct((chunk // 2, width), F32), gain, gain, struct((1, 1), F32)),
+        in_specs=[anywhere] * 3 + [vmem] * 4,
+        out_specs=(anywhere, anywhere, anywhere, vmem, vmem, vmem, vmem),
+        scratch_shapes=[pltpu.VMEM((3, 2, tokens // 2, inner), BF16), dma((3, 2)), dma((3, 2))],
+        name="write",
+    )(dq, dk, dv, weight_grad, qgain, kgain, norm)
     return (
         dq[None],
         dk[None],
         dv[None],
-        weight_grad,
+        weight_grad.T,
         qgain.reshape(HEAD_DIM),
         kgain.reshape(HEAD_DIM),
         norm.reshape(()),

time: 265 us -> 253 us (0.955)
  local copies, waits for them, and re-layouts: 9.08 us -> 0 us
    unnamed x10 -> x0, local copies, waits for them, and re-layouts: 9.08 us -> none
    pallas_call x1, Pallas kernels: 253 us -> 248 us  [local(): pl.pallas_call(functools.partial(kernel, n, side), out_shape=(struct((tok...]
    pallas_call x0 -> x1, Pallas kernels: none -> 4.85 us  [local(): pl.pallas_call(write_kernel, out_shape=(rows, rows, rows, struct((chunk /...]
where the time goes in v3:
time: 253 us
  Pallas kernels  252 us (100%)
    pallas_call x1, Pallas kernels, local(): pl.pallas_call(functools.partial(kernel, n, side), out_shape=(struct((tok...  248 us

profile of v3, /device:TPU:1, one launch (start us, length us, event | category | flops | bytes accessed | tf_op | source)
XLA Modules:
  0.0 253.1 jit_solution(13724401151604508802)
XLA Ops:
  0.6 247.6 %fused.1 = (bf16[128,3072]{1,0:T(8,128)(2,1)}, bf16[128,3072]{1,0:T(8,128)(2,1)}, bf16[128,3072]{1,0:T(8,128)(2,1)}, f32[384,192]{1,0:T(8,128)}, f32[1,128]{1,0:...) custom-call(bf16[128,3072]{1,0:T(8,128)(2,1)} %bitcast.15, bf16[128,3072]{1,0:T(8,128)(2,1)} %bitcast.16, ...), custom_call_target="tpu_custom_call" | custom-call | tf_op jit(solution)/shard_map/fused/pallas_call | solution.py:564
  248.2 4.8 %write.1 = (bf16[128,3072]{1,0:T(8,128)(2,1)}, bf16[128,3072]{1,0:T(8,128)(2,1)}, bf16[128,3072]{1,0:T(8,128)(2,1)}, f32[192,384]{1,0:T(8,128)}, f32[1,128]{1,0:...) custom-call(bf16[128,3072]{1,0:T(8,128)(2,1)} %get-tuple-element.21.dq_in, bf16[128,3072]{1,0:T(8,128)(2,1)} %get-tuple-element.22.dk_in, ...), custom_call_target="tpu_custom_call" | custom-call | tf_op jit(solution)/shard_map/write/pallas_call | solution.py:637

commit v4 on v2

--- a/solution.py
+++ b/solution.py
@@ -48,9 +48,7 @@
     dk_out,
     dv_out,
     w_out,
-    qgain_out,
-    kgain_out,
-    norm_out,
+    small_out,
     qkv,
     kn,
     knt,
@@ -70,10 +68,13 @@
     theirs,
     packed,
     slots,
+    part,
+    second,
     reduced,
     final,
     z_slots,
-    dp_slots,
+    row_slots,
+    y_slots,
     qkv_send,
     qkv_recv,
     ag_send,
@@ -84,14 +85,18 @@
     dkv_recv,
     swap_send,
     swap_recv,
-    x_send,
-    x_recv,
+    first_send,
+    first_recv,
+    second_send,
+    second_recv,
     last_send,
     last_recv,
     z_send,
     z_recv,
-    dp_send,
-    dp_recv,
+    row_send,
+    row_recv,
+    y_send,
+    y_recv,
     own_sem,
 ):
     me = lax.axis_index("seq")
@@ -113,9 +118,8 @@
     chunk = model // chips
     per_sub = chips // SUBS
     half = width // 2
-    here = y * side + x
-    group = 2 * chips
-    in_group = here * 2 + core
+    in_row = x * 2 + core
+    home = lax.rem(x + y, side)
 
     def columns(index):
         return pl.ds(pl.multiple_of(index * width, width), width)
@@ -135,17 +139,17 @@
     def z_peer(d):
         return {"seq": peer(d)}, peer(d)
 
-    def chip(d):
-        place = lax.rem(here + d, chips)
-        return {"dp_0": place // side, "dp_1": lax.rem(place, side)}, place
-
-    def dp_peer(d):
-        place = lax.rem(in_group + d, group)
-        return {
-            "dp_0": place // (2 * side),
-            "dp_1": lax.rem(place // 2, side),
-            "dp_2": lax.rem(place, 2),
-        }, place
+    def row_peer(d):
+        place = lax.rem(in_row + d, 2 * side)
+        return {"dp_1": place // 2, "dp_2": lax.rem(place, 2)}, place
+
+    def y_peer(d):
+        place = lax.rem(y + d, side)
+        return {"dp_0": place}, place
+
+    def x_peer(d):
+        place = lax.rem(x + d, side)
+        return {"dp_1": place}, place
 
     def remote(src, dst, send, recv, to):
         return pltpu.make_async_remote_copy(
@@ -155,21 +159,42 @@
     barrier = pltpu.get_barrier_semaphore()
     for d in range(1, n):
         pl.semaphore_signal(barrier, inc=1, device_id=z_peer(d)[0], device_id_type=MESH)
-    for d in range(1, group):
-        pl.semaphore_signal(barrier, inc=1, device_id=dp_peer(d)[0], device_id_type=MESH)
+    for d in range(1, 2 * side):
+        pl.semaphore_signal(barrier, inc=1, device_id=row_peer(d)[0], device_id_type=MESH)
+    for d in range(1, side):
+        pl.semaphore_signal(barrier, inc=1, device_id=y_peer(d)[0], device_id_type=MESH)
 
     own_copies = [
         pltpu.make_async_copy(ref.at[:, columns(me)], qkv.at[i, rows_of(me)], own_sem.at[i])
         for i, ref in enumerate((q_hbm, k_hbm, v_hbm))
     ]
+    def chunk_at(sub, j):
+        return side * j + lax.rem(sub - j + side, side)
+
+    def chunk_of(index):
+        return pl.ds(pl.multiple_of(index * chunk, chunk), chunk)
+
     do_copies = [
-        pltpu.make_async_copy(do_hbm.at[:, sub_of(sub)], do_all.at[me, sub], own_sem.at[4 + sub])
+        pltpu.make_async_copy(
+            do_hbm.at[:, chunk_of(chunk_at(sub, j))],
+            do_all.at[me, sub, :, pl.ds(j * chunk, chunk)],
+            own_sem.at[4 + sub * per_sub + j],
+        )
         for sub in range(SUBS)
+        for j in range(per_sub)
     ]
-    w_copy = pltpu.make_async_copy(w_hbm, w, own_sem.at[3])
-    for copy in own_copies + do_copies + [w_copy]:
+    w_copies = [
+        pltpu.make_async_copy(
+            w_hbm.at[:, chunk_of(chunk_at(sub, j))],
+            w.at[:, pl.ds((sub * per_sub + j) * chunk, chunk)],
+            own_sem.at[4 + chips + sub * per_sub + j],
+        )
+        for sub in range(SUBS)
+        for j in range(per_sub)
+    ]
+    for copy in do_copies + own_copies + w_copies:
         copy.start()
-    pl.semaphore_wait(barrier, n + group - 2)
+    pl.semaphore_wait(barrier, n + 3 * side - 3)
 
     order = [4, 3, 5, 2, 6, 1, 7] if n == 8 else list(range(1, n))
     arrays = ((1, k_hbm), (2, v_hbm), (0, q_hbm))
@@ -188,18 +213,20 @@
         for d in order:
             qkv_copy(i, ref, d, me).start()
 
-    def ring(direction, step, sub, block, to, own=False):
+    def ring(direction, step, sub, block, to):
         return remote(
-            do_hbm.at[:, sub_of(sub)] if own else do_all.at[block, sub],
+            do_all.at[block, sub],
             do_all.at[block, sub],
             ag_send.at[direction, step, sub],
             ag_recv.at[block, sub],
             {"seq": to},
         )
 
+    for copy in do_copies:
+        copy.wait()
     for sub in range(SUBS):
-        ring(0, 0, sub, me, up, True).start()
-        ring(1, 0, sub, me, down, True).start()
+        ring(0, 0, sub, me, up).start()
+        ring(1, 0, sub, me, down).start()
 
     dkt[...] = jnp.zeros(dkt.shape, F32)
     dvt[...] = jnp.zeros(dvt.shape, F32)
@@ -214,6 +241,14 @@
     qg = qg_ref[...]
     seg_k = seg_of(lax.broadcasted_iota(jnp.int32, (1, total), 1), lengths_ref)
 
+    def project(t, sub):
+        term = dot(do_all[t, sub], w[:, sub_of(sub)], NT)
+        datt[t] = term if sub == 0 else datt[t] + term
+
+    for copy in w_copies:
+        copy.wait()
+    for sub in range(SUBS):
+        project(me, sub)
     for copy in own_copies:
         copy.wait()
     for i, ref in arrays:
@@ -258,13 +293,6 @@
         return carry
 
     lax.fori_loop(0, total // 256, forward, 0)
-    for copy in do_copies:
-        copy.wait()
-    w_copy.wait()
-
-    def project(t, sub):
-        part = sub_of(sub)
-        datt[...] += dot(do_all[t, sub], w[:, part], NT)
 
     def weigh(t, sub):
         def piece(j, c):
@@ -280,7 +308,7 @@
         cols = pl.ds(h * HEAD_DIM, HEAD_DIM)
         unit, inverse = norm_rows(0, rows, cols)
         normed = unit * qg
-        dattn = datt[:, cols]
+        dattn = datt[t, :, cols]
         prob = probs[h, rows, :]
         prob32 = prob.astype(F32)
         d_probs = dot(dattn.astype(BF16), vt[cols, :])
@@ -297,47 +325,50 @@
             dqs.at[t], dq_out.at[:, columns(place)], dq_send.at[t], dq_recv.at[place], {"seq": t}
         )
 
-    def body(i, carry):
-        step = (i + 1) // 2
-        odd = lax.rem(i, 2)
-        shift = sign * step
-        t = lax.rem(me + shift - 2 * odd * shift + n, n)
-        a_block = lax.rem(me - shift + n, n)
-        b_block = lax.rem(me + shift + n, n)
-
-        @pl.when(odd == 1)
-        def _():
-            for sub in range(SUBS):
-                ring(0, step - 1, sub, a_block, up).wait_recv()
-                ring(0, step, sub, a_block, up).start()
-            for sub in range(SUBS):
-                ring(1, step - 1, sub, b_block, down).wait_recv()
-
-                @pl.when(step < b_steps)
+    def block_at(shift):
+        return lax.rem(me + sign * shift + n, n)
+
+    for sub in range(SUBS):
+        weigh(me, sub)
+
+    def body(step, carry):
+        a_block = block_at(-step)
+        b_block = block_at(step)
+        a_last = block_at(1 - step)
+        b_last = block_at(step - 1)
+        for sub in range(SUBS):
+            ring(0, step - 1, sub, a_block, up).wait_recv()
+            ring(0, step, sub, a_block, up).start()
+            ring(1, step - 1, sub, b_block, down).wait_recv()
+
+            @pl.when(step < b_steps)
+            def _():
+                ring(1, step, sub, b_block, down).start()
+
+            for block in (a_block, b_block):
+                project(block, sub)
+                weigh(block, sub)
+            if sub == 0:
+                backward(a_last, 0)
+            elif sub == 1:
+                for h in range(1, heads):
+                    backward(a_last, h)
+            else:
+
+                @pl.when(step > 1)
                 def _():
-                    ring(1, step, sub, b_block, down).start()
-
-        datt[...] = jnp.zeros(datt.shape, F32)
-        for sub in range(SUBS):
-            project(t, sub)
-        for h in range(heads):
-            backward(t, h)
-
-        @pl.when(i > 0)
-        def _():
-            dq_copy(t, me).start()
-
-        for sub in range(SUBS):
-            weigh(t, sub)
+                    for h in (0,) if sub == 2 else range(1, heads):
+                        backward(b_last, h)
+
         return carry
 
-    lax.fori_loop(0, n - 1, body, 0)
-
+    lax.fori_loop(1, a_steps, body, 0)
     own_dq = pltpu.make_async_copy(dqs.at[me], dq_out.at[:, columns(me)], own_sem.at[0])
     own_dq.start()
 
-    t = lax.rem(me - sign * a_steps + n, n)
-    datt[...] = jnp.zeros(datt.shape, F32)
+    t = block_at(-a_steps)
+    a_last = block_at(-b_steps)
+    b_last = block_at(b_steps)
 
     def swap(sub):
         part = sub_of(sub)
@@ -349,45 +380,65 @@
             {"dp_2": other},
         )
 
-    def scatter(d, place_here):
-        target, place = chip(d)
+    def held_at(sub, place):
+        return chunk_at(sub, lax.rem(sub - place + side, side)) if sub % 2 == 0 else chunk_at(sub, place)
+
+    def first_copy(sub, d, source):
+        to, place = x_peer(d) if sub % 2 == 0 else y_peer(d)
         return remote(
-            packed.at[place], slots.at[place_here], x_send.at[place], x_recv.at[place_here], target
-        )
+            packed.at[held_at(sub, place)],
+            slots.at[sub, source],
+            first_send.at[sub, d],
+            first_recv.at[sub, source],
+            to,
+        )
+
+    def first_sends(sub):
+        for d in range(1, side):
+            first_copy(sub, d, x if sub % 2 == 0 else y).start()
+
+    def second_copy(sub):
+        owner = lax.rem(sub - (x if sub % 2 == 0 else y) + side, side)
+        source = y if sub % 2 == 0 else x
+        return remote(
+            part.at[sub],
+            second.at[source],
+            second_send.at[sub],
+            second_recv.at[source],
+            {"dp_0": owner} if sub % 2 == 0 else {"dp_1": owner},
+        )
+
+    def combine(sub):
+        whole = packed[held_at(sub, x if sub % 2 == 0 else y)].astype(F32)
+        for d in range(1, side):
+            source = (x_peer(d) if sub % 2 == 0 else y_peer(d))[1]
+            first_copy(sub, d, source).wait_recv()
+            whole = whole + slots[sub, source].astype(F32)
+        part[sub] = whole.astype(BF16)
+
+    def second_sends(sub):
+        @pl.when(home != sub)
+        def _():
+            second_copy(sub).start()
 
     def merge(sub):
         swap(sub).wait_recv()
 
         def piece(j, carry):
-            part = pl.ds(pl.multiple_of(j * chunk, chunk), chunk)
-            packed[j] = (wpb[half_of(core), part].astype(F32) + theirs[:, part].astype(F32)).astype(BF16)
+            part = chunk_of(sub * per_sub + j)
+            whole = wpb[half_of(core), part].astype(F32) + theirs[:, part].astype(F32)
+            packed[chunk_at(sub, j)] = whole.astype(BF16)
             return carry
 
-        lax.fori_loop(sub * per_sub, (sub + 1) * per_sub, piece, 0)
-
-    def scatter_of(place):
-        return remote(
-            packed.at[place],
-            slots.at[here],
-            x_send.at[place],
-            x_recv.at[here],
-            {"dp_0": place // side, "dp_1": lax.rem(place, side)},
-        )
-
-    def send_sub(sub):
-        def one(j, carry):
-            place = sub * per_sub + lax.rem(here + j, per_sub)
-
-            @pl.when(place != here)
-            def _():
-                scatter_of(place).start()
-
-            return carry
-
-        lax.fori_loop(0, per_sub, one, 0)
+        lax.fori_loop(0, per_sub, piece, 0)
 
     for sub in range(SUBS):
         ring(0, a_steps - 1, sub, t, up).wait_recv()
+        if sub == SUBS - 1:
+            for step in range(1, b_steps):
+                dq_copy(block_at(-step), me).start()
+                dq_copy(block_at(step), me).start()
+            dq_copy(a_last, me).start()
         weigh(t, sub)
 
         def narrow(j, carry, sub=sub):
@@ -396,13 +447,15 @@
             return carry
 
         lax.fori_loop(0, quarter // 512, narrow, 0)
+        swap(sub).start()
+        project(t, sub)
+        merge(sub)
+        first_sends(sub)
         if sub > 0:
-            merge(sub - 1)
-        project(t, sub)
-        swap(sub).start()
-        if sub > 0:
-            send_sub(sub - 1)
-
+            combine(sub - 1)
+            second_sends(sub - 1)
+        if sub < heads:
+            backward(a_last, sub)
     def dkv_copy(i, h, d, place):
         to = peer(d)
         return remote(
@@ -415,6 +468,7 @@
 
     for h in range(heads):
         cols = pl.ds(h * HEAD_DIM, HEAD_DIM)
+        backward(b_last, h)
         backward(t, h)
 
         def finish(j, carry, cols=cols):
@@ -427,12 +481,13 @@
             return carry
 
         lax.fori_loop(0, total // 256, finish, 0)
-        for i in (1, 0):
+        for i in (1, 0) if h < heads - 1 else (1,):
             for d in order:
                 dkv_copy(i, h, d, me).start()
         if h == 0:
-            merge(SUBS - 1)
-            send_sub(SUBS - 1)
+            combine(SUBS - 1)
+            second_sends(SUBS - 1)
+    dq_copy(b_last, me).start()
     dq_copy(t, me).start()
     own_dkv = [
         pltpu.make_async_copy(dkv.at[i, rows_of(me)], out.at[:, columns(me)], own_sem.at[1 + i])
@@ -441,11 +496,12 @@
     for copy in own_dkv:
         copy.start()
 
-    reduced[...] = packed[here].astype(F32)
-    for d in range(1, chips):
-        place = chip(d)[1]
-        scatter(d, place).wait_recv()
-        reduced[...] += slots[place].astype(F32)
+    reduced[...] = part[home].astype(F32)
+    start = jnp.where(lax.rem(home, 2) == 0, y, x)
+    for d in range(1, side):
+        source = lax.rem(start + d, side)
+        remote(part.at[0], second.at[source], second_send.at[0], second_recv.at[source], x_peer(1)[0]).wait_recv()
+        reduced[...] += second[source].astype(F32)
 
     def window(index):
         return pl.ds(pl.multiple_of(index * 128, 128), 256)
@@ -457,22 +513,23 @@
     def pick(block):
         return jnp.where(core == 0, block[:, :shard_width], block[:, 256 - shard_width :])
 
-    mine = pick(reduced[:, window(core)])
-    w_out[half_of(core), :] = mine
-    square = jnp.sum(mine * mine)
+    square = jnp.sum(reduced[...] * reduced[...])
     row = lax.broadcasted_iota(jnp.int32, (8, 128), 0)
-    last.wait_recv()
-    rest = pick(final[...])
-    w_out[half_of(other), :] = rest
-    square = square + jnp.sum(rest * rest)
-    z_slots[me] = jnp.where(row == 2, square, gain[...])
-
-    def spread(buffer, peers, count, sends, recvs, place):
+    row_slots[in_row] = jnp.where(row == 2, square, gain[...])
+    w_out[half_of(core), :] = pick(reduced[:, window(core)])
+
+    def rest_of_dk():
+        for d in order:
+            dkv_copy(0, heads - 1, d, me).start()
+
+    def spread(buffer, peers, count, sends, recvs, place, then=None):
         def copy(d, source):
             return remote(buffer.at[source], buffer.at[source], sends.at[d], recvs.at[source], peers(d)[0])
 
         for d in range(1, count):
             copy(d, place).start()
+        if then is not None:
+            then()
         for d in range(1, count):
             copy(d, peers(d)[1]).wait_recv()
         result = buffer[0]
@@ -482,15 +539,16 @@
             copy(d, place).wait_send()
         return result
 
-    dp_slots[in_group] = spread(z_slots, z_peer, n, z_send, z_recv, me)
-    summed = spread(dp_slots, dp_peer, group, dp_send, dp_recv, in_group)
+    y_slots[y] = spread(row_slots, row_peer, 2 * side, row_send, row_recv, in_row)
+    z_slots[me] = spread(y_slots, y_peer, side, y_send, y_recv, y)
+    last.wait_recv()
+    w_out[half_of(other), :] = pick(final[...])
+    summed = spread(z_slots, z_peer, n, z_send, z_recv, me, rest_of_dk)
     gains = jnp.where(row < 2, summed, 0.0)
     squares = summed[2:3, 0:1] + jnp.sum(gains * gains)
     norm = jnp.sqrt(squares)
     factor = jnp.minimum(1.0, MAX_NORM / (norm + EPS))
-    qgain_out[...] = gains[0:1] * factor
-    kgain_out[...] = gains[1:2] * factor
-    norm_out[...] = norm
+    small_out[...] = jnp.where(row < 2, gains * factor, norm)
     w_out[...] = w_out[...] * factor
 
     last.wait_send()
@@ -506,8 +564,13 @@
             ring(0, step, sub, me, up).wait_send()
         for step in range(b_steps):
             ring(1, step, sub, me, down).wait_send()
-    for d in range(1, chips):
-        scatter(d, here).wait_send()
+        for d in range(1, side):
+            first_copy(sub, d, 0).wait_send()
+
+        @pl.when(home != sub)
+        def _():
+            second_copy(sub).wait_send()
+
     for d in range(1, n):
         dq_copy(peer(d), me).wait_send()
         dq_copy(peer(d), peer(d)).wait_recv()
@@ -515,6 +578,35 @@
             for h in range(heads):
                 dkv_copy(i, h, d, me).wait_send()
                 dkv_copy(i, h, d, peer(d)).wait_recv()
+
+
+def write_kernel(
+    dq_in, dk_in, dv_in, w_in, small_in, dq_out, dk_out, dv_out, w_out, qgain_out, kgain_out, norm_out,
+    rows, block, turned, small, norm, in_sem, out_sem,
+):
+    loads = [pltpu.make_async_copy(w_in, block, in_sem.at[3]), pltpu.make_async_copy(small_in, small, in_sem.at[4])]
+    for i, ref in enumerate((dq_in, dk_in, dv_in)):
+        loads.append(pltpu.make_async_copy(ref, rows.at[i], in_sem.at[i]))
+    for load in loads:
+        load.start()
+    stores = [
+        pltpu.make_async_copy(small.at[0:1], qgain_out, out_sem.at[3]),
+        pltpu.make_async_copy(small.at[1:2], kgain_out, out_sem.at[4]),
+        pltpu.make_async_copy(norm, norm_out, out_sem.at[5]),
+        pltpu.make_async_copy(turned, w_out, out_sem.at[6]),
+    ]
+    loads[0].wait()
+    loads[1].wait()
+    norm[...] = small[2:3, :]
+    turned[...] = jnp.transpose(block[...])
+    for i, ref in enumerate((dq_out, dk_out, dv_out)):
+        loads[2 + i].wait()
+        stores.append(pltpu.make_async_copy(rows.at[i], ref, out_sem.at[i]))
+        stores[-1].start()
+    for store in stores[:4]:
+        store.start()
+    for store in stores:
+        store.wait()
 
 
 def local(n, side, query_rows, key_rows, value_rows, out_grad, clip_lengths, out_weight, query_gain, key_gain):
@@ -530,19 +622,17 @@
     struct = jax.ShapeDtypeStruct
     chips = side * side
     chunk = model // chips
-    dq, dk, dv, weight_grad, qgain, kgain, norm = pl.pallas_call(
+    dq, dk, dv, weight_grad, small = pl.pallas_call(
         functools.partial(kernel, n, side),
         out_shape=(
             struct((tokens, inner), BF16),
             struct((tokens, inner), BF16),
             struct((tokens, inner), BF16),
             struct((width, chunk // 2), F32),
-            struct((1, HEAD_DIM), F32),
-            struct((1, HEAD_DIM), F32),
-            struct((1, 1), F32),
+            struct((8, HEAD_DIM), F32),
         ),
         in_specs=[anywhere] * 5 + [smem, vmem, vmem],
-        out_specs=(anywhere, anywhere, anywhere, vmem, vmem, vmem, vmem),
+        out_specs=(anywhere, anywhere, anywhere, vmem, vmem),
         scratch_shapes=[
             pltpu.VMEM((3, total, width), BF16),
             pltpu.VMEM((total, width), BF16),
@@ -553,7 +643,7 @@
             pltpu.VMEM((width, model), F32),
             pltpu.VMEM((width, total), F32),
             pltpu.VMEM((width, total), F32),
-            pltpu.VMEM((tokens, width), F32),
+            pltpu.VMEM((n, tokens, width), F32),
             pltpu.VMEM((width, total), BF16),
             pltpu.VMEM((heads, total, total), BF16),
             pltpu.VMEM((n, tokens, width), BF16),
@@ -562,11 +652,14 @@
             pltpu.VMEM((width, model), BF16),
             pltpu.VMEM((width // 2, model), BF16),
             pltpu.VMEM((chips, width // 2, chunk), BF16),
-            pltpu.VMEM((chips, width // 2, chunk), BF16),
+            pltpu.VMEM((SUBS, side, width // 2, chunk), BF16),
+            pltpu.VMEM((SUBS, width // 2, chunk), BF16),
+            pltpu.VMEM((side, width // 2, chunk), BF16),
             pltpu.VMEM((width // 2, chunk), F32),
             pltpu.VMEM((width // 2, 256), F32),
             pltpu.VMEM((n, 8, 128), F32),
-            pltpu.VMEM((2 * chips, 8, 128), F32),
+            pltpu.VMEM((2 * side, 8, 128), F32),
+            pltpu.VMEM((side, 8, 128), F32),
             dma((3, n)),
             dma((3, n)),
             dma((2, n // 2, SUBS)),
@@ -577,15 +670,19 @@
             dma((2, heads, n)),
             dma((SUBS,)),
             dma((SUBS,)),
-            dma((chips,)),
-            dma((chips,)),
+            dma((SUBS, side)),
+            dma((SUBS, side)),
+            dma((SUBS,)),
+            dma((side,)),
             dma((1,)),
             dma((1,)),
             dma((n,)),
             dma((n,)),
-            dma((2 * chips,)),
-            dma((2 * chips,)),
-            dma((8,)),
+            dma((2 * side,)),
+            dma((2 * side,)),
+            dma((side,)),
+            dma((side,)),
+            dma((4 + 2 * chips,)),
         ],
         compiler_params=pltpu.CompilerParams(
             collective_id=1, has_side_effects=True, vmem_limit_bytes=67043328
@@ -601,14 +698,32 @@
         query_gain[None],
         key_gain[None],
     )
+    rows = struct((tokens, inner), BF16)
+    gain = struct((1, HEAD_DIM), F32)
+    dq, dk, dv, weight_grad, qgain, kgain, norm = pl.pallas_call(
+        write_kernel,
+        out_shape=(rows, rows, rows, struct((chunk // 2, width), F32), gain, gain, gain),
+        in_specs=[anywhere] * 5,
+        out_specs=(anywhere,) * 7,
+        scratch_shapes=[
+            pltpu.VMEM((3, tokens, inner), BF16),
+            pltpu.VMEM((width, chunk // 2), F32),
+            pltpu.VMEM((chunk // 2, width), F32),
+            pltpu.VMEM((8, HEAD_DIM), F32),
+            pltpu.VMEM((1, HEAD_DIM), F32),
+            dma((5,)),
+            dma((7,)),
+        ],
+        name="write",
+    )(dq, dk, dv, weight_grad, small)
     return (
         dq[None],
         dk[None],
         dv[None],
-        weight_grad,
+        weight_grad.T,
         qgain.reshape(HEAD_DIM),
         kgain.reshape(HEAD_DIM),
-        norm.reshape(()),
+        norm[0, 0],
     )
 
 

time: 265 us -> 247 us (0.932)
  local copies, waits for them, and re-layouts: 9.08 us -> 0 us
  Pallas kernels: 253 us -> 246 us
    pallas_call x1, Pallas kernels: 253 us -> 243 us  [local(): pl.pallas_call(functools.partial(kernel, n, side), out_shape=(struct((tok...]
    unnamed x10 -> x0, local copies, waits for them, and re-layouts: 9.08 us -> none
    pallas_call x0 -> x1, Pallas kernels: none -> 2.87 us  [local(): pl.pallas_call(write_kernel, out_shape=(rows, rows, rows, struct((chunk /...]
where the time goes in v4:
time: 247 us; the launch traced here: 246 us
  Pallas kernels  246 us (100%)
    pallas_call x1, Pallas kernels, local(): pl.pallas_call(functools.partial(kernel, n, side), out_shape=(struct((tok...  243 us

profile of v4, /device:TPU:1, one launch (start us, length us, event | category | flops | bytes accessed | tf_op | source)
XLA Modules:
  0.0 246.4 jit_solution(16577633605951267723)
XLA Ops:
  0.6 242.7 %fused.1 = (bf16[128,3072]{1,0:T(8,128)(2,1)}, bf16[128,3072]{1,0:T(8,128)(2,1)}, bf16[128,3072]{1,0:T(8,128)(2,1)}, f32[384,192]{1,0:T(8,128)}, f32[8,128]{1,0:T(8,128)}) custom-call(bf16[128,3072]{1,0:T(8,128)(2,1)} %bitcast.16, bf16[128,3072]{1,0:T(8,128)(2,1)} %bitcast.17, bf16[128,3072]{1,0:T(8,128)(2,1)} %bitcast.18, bf16[128,6144]{1,0:T(8,128)(2,1)} %bitcast.15, ...), custom_call_target="tpu_custom_call" | custom-call | tf_op jit(solution)/shard_map/fused/pallas_call | solution.py:625
  243.4 2.9 %write.1 = (bf16[128,3072]{1,0:T(8,128)(2,1)}, bf16[128,3072]{1,0:T(8,128)(2,1)}, bf16[128,3072]{1,0:T(8,128)(2,1)}, f32[192,384]{1,0:T(8,128)}, f32[1,128]{1,0:...) custom-call(bf16[128,3072]{1,0:T(8,128)(2,1)} %get-tuple-element.19.dq_in, bf16[128,3072]{1,0:T(8,128)(2,1)} %get-tuple-element.20.dk_in, ...), custom_call_target="tpu_custom_call" | custom-call | tf_op jit(solution)/shard_map/write/pallas_call | solution.py:703

commit v5 on v4

--- a/solution.py
+++ b/solution.py
@@ -41,12 +41,16 @@
     v_hbm,
     do_hbm,
     w_hbm,
-    lengths_ref,
-    qg_ref,
-    kg_ref,
+    lengths_hbm,
+    qg_hbm,
+    kg_hbm,
     dq_out,
     dk_out,
     dv_out,
+    w_hbm_out,
+    small_hbm_out,
+    lengths_ref,
+    gains_in,
     w_out,
     small_out,
     qkv,
@@ -192,7 +196,12 @@
         for sub in range(SUBS)
         for j in range(per_sub)
     ]
-    for copy in do_copies + own_copies + w_copies:
+    small_copies = [
+        pltpu.make_async_copy(lengths_hbm, lengths_ref, own_sem.at[4 + 2 * chips]),
+        pltpu.make_async_copy(qg_hbm, gains_in.at[0:1], own_sem.at[5 + 2 * chips]),
+        pltpu.make_async_copy(kg_hbm, gains_in.at[1:2], own_sem.at[6 + 2 * chips]),
+    ]
+    for copy in do_copies + own_copies + small_copies + w_copies:
         copy.start()
     pl.semaphore_wait(barrier, n + 3 * side - 3)
 
@@ -237,8 +246,10 @@
         return carry
 
     lax.fori_loop(0, model // 512, clear, 0)
-    kg = kg_ref[...]
-    qg = qg_ref[...]
+    for copy in small_copies:
+        copy.wait()
+    qg = gains_in[0:1]
+    kg = gains_in[1:2]
     seg_k = seg_of(lax.broadcasted_iota(jnp.int32, (1, total), 1), lengths_ref)
 
     def project(t, sub):
@@ -550,10 +561,15 @@
     factor = jnp.minimum(1.0, MAX_NORM / (norm + EPS))
     small_out[...] = jnp.where(row < 2, gains * factor, norm)
     w_out[...] = w_out[...] * factor
-
     last.wait_send()
+    results = [
+        pltpu.make_async_copy(small_out, small_hbm_out, own_sem.at[5 + 2 * chips]),
+        pltpu.make_async_copy(w_out, w_hbm_out, own_sem.at[6 + 2 * chips]),
+    ]
+    for copy in results:
+        copy.start()
     own_dq.wait()
-    for copy in own_dkv:
+    for copy in own_dkv + results:
         copy.wait()
     for i, ref in arrays:
         for d in order:
@@ -584,27 +600,30 @@
     dq_in, dk_in, dv_in, w_in, small_in, dq_out, dk_out, dv_out, w_out, qgain_out, kgain_out, norm_out,
     rows, block, turned, small, norm, in_sem, out_sem,
 ):
-    loads = [pltpu.make_async_copy(w_in, block, in_sem.at[3]), pltpu.make_async_copy(small_in, small, in_sem.at[4])]
-    for i, ref in enumerate((dq_in, dk_in, dv_in)):
-        loads.append(pltpu.make_async_copy(ref, rows.at[i], in_sem.at[i]))
+    loads = [pltpu.make_async_copy(w_in, block, in_sem.at[0]), pltpu.make_async_copy(small_in, small, in_sem.at[1])]
+    half = rows.shape[1] // 2
+    pieces = [(i, pl.ds(p * half, half), 2 * i + p) for i in range(3) for p in range(2)]
+    ins, outs = (dq_in, dk_in, dv_in), (dq_out, dk_out, dv_out)
+    for i, part, k in pieces:
+        loads.append(pltpu.make_async_copy(ins[i].at[part], rows.at[i, part], in_sem.at[2 + k]))
     for load in loads:
         load.start()
     stores = [
-        pltpu.make_async_copy(small.at[0:1], qgain_out, out_sem.at[3]),
-        pltpu.make_async_copy(small.at[1:2], kgain_out, out_sem.at[4]),
-        pltpu.make_async_copy(norm, norm_out, out_sem.at[5]),
-        pltpu.make_async_copy(turned, w_out, out_sem.at[6]),
+        pltpu.make_async_copy(small.at[0:1], qgain_out, out_sem.at[0]),
+        pltpu.make_async_copy(small.at[1:2], kgain_out, out_sem.at[1]),
+        pltpu.make_async_copy(norm, norm_out, out_sem.at[2]),
+        pltpu.make_async_copy(turned, w_out, out_sem.at[3]),
     ]
     loads[0].wait()
     loads[1].wait()
     norm[...] = small[2:3, :]
     turned[...] = jnp.transpose(block[...])
-    for i, ref in enumerate((dq_out, dk_out, dv_out)):
-        loads[2 + i].wait()
-        stores.append(pltpu.make_async_copy(rows.at[i], ref, out_sem.at[i]))
+    for store in stores:
+        store.start()
+    for i, part, k in pieces:
+        loads[2 + k].wait()
+        stores.append(pltpu.make_async_copy(rows.at[i, part], outs[i].at[part], out_sem.at[4 + k]))
         stores[-1].start()
-    for store in stores[:4]:
-        store.start()
     for store in stores:
         store.wait()
 
@@ -615,8 +634,6 @@
     width = inner // n
     heads = width // HEAD_DIM
     total = tokens * n
-    vmem = pl.BlockSpec(memory_space=pltpu.VMEM)
-    smem = pl.BlockSpec(memory_space=pltpu.SMEM)
     anywhere = pl.BlockSpec(memory_space=pl.ANY)
     dma = pltpu.SemaphoreType.DMA
     struct = jax.ShapeDtypeStruct
@@ -631,9 +648,13 @@
             struct((width, chunk // 2), F32),
             struct((8, HEAD_DIM), F32),
         ),
-        in_specs=[anywhere] * 5 + [smem, vmem, vmem],
-        out_specs=(anywhere, anywhere, anywhere, vmem, vmem),
+        in_specs=[anywhere] * 8,
+        out_specs=(anywhere,) * 5,
         scratch_shapes=[
+            pltpu.SMEM(clip_lengths.shape[1:], jnp.int32),
+            pltpu.VMEM((8, HEAD_DIM), F32),
+            pltpu.VMEM((width, chunk // 2), F32),
+            pltpu.VMEM((8, HEAD_DIM), F32),
             pltpu.VMEM((3, total, width), BF16),
             pltpu.VMEM((total, width), BF16),
             pltpu.VMEM((width, total), BF16),
@@ -682,7 +703,7 @@
             dma((2 * side,)),
             dma((side,)),
             dma((side,)),
-            dma((4 + 2 * chips,)),
+            dma((7 + 2 * chips,)),
         ],
         compiler_params=pltpu.CompilerParams(
             collective_id=1, has_side_effects=True, vmem_limit_bytes=67043328
@@ -711,8 +732,8 @@
             pltpu.VMEM((chunk // 2, width), F32),
             pltpu.VMEM((8, HEAD_DIM), F32),
             pltpu.VMEM((1, HEAD_DIM), F32),
-            dma((5,)),
-            dma((7,)),
+            dma((8,)),
+            dma((10,)),
         ],
         name="write",
     )(dq, dk, dv, weight_grad, small)

time: 247 us -> 245 us (level)
  no operation moved by 1% of the time
where the time goes in v5:
time: 245 us
  Pallas kernels  244 us (100%)
    pallas_call x1, Pallas kernels, local(): pl.pallas_call(functools.partial(kernel, n, side), out_shape=(struct((tok...  241 us

profile of v5, /device:TPU:1, one launch (start us, length us, event | category | flops | bytes accessed | tf_op | source)
XLA Modules:
  0.0 244.9 jit_solution(2297303402150980709)
XLA Ops:
  0.6 241.3 %fused.1 = (bf16[128,3072]{1,0:T(8,128)(2,1)}, bf16[128,3072]{1,0:T(8,128)(2,1)}, bf16[128,3072]{1,0:T(8,128)(2,1)}, f32[384,192]{1,0:T(8,128)}, f32[8,128]{1,0:T(8,128)}) custom-call(bf16[128,3072]{1,0:T(8,128)(2,1)} %bitcast.16, bf16[128,3072]{1,0:T(8,128)(2,1)} %bitcast.17, bf16[128,3072]{1,0:T(8,128)(2,1)} %bitcast.18, bf16[128,6144]{1,0:T(8,128)(2,1)} %bitcast.15, ...), custom_call_target="tpu_custom_call" | custom-call | tf_op jit(solution)/shard_map/fused/pallas_call | solution.py:642
  242.0 2.8 %write.1 = (bf16[128,3072]{1,0:T(8,128)(2,1)}, bf16[128,3072]{1,0:T(8,128)(2,1)}, bf16[128,3072]{1,0:T(8,128)(2,1)}, f32[192,384]{1,0:T(8,128)}, f32[1,128]{1,0:...) custom-call(bf16[128,3072]{1,0:T(8,128)(2,1)} %get-tuple-element.19.dq_in, bf16[128,3072]{1,0:T(8,128)(2,1)} %get-tuple-element.20.dk_in, ...), custom_call_target="tpu_custom_call" | custom-call | tf_op jit(solution)/shard_map/write/pallas_call | solution.py:724

commit v6 on v5

--- a/solution.py
+++ b/solution.py
@@ -462,7 +462,7 @@
         project(t, sub)
         merge(sub)
         first_sends(sub)
-        if sub > 0:
+        if 0 < sub < SUBS - 1:
             combine(sub - 1)
             second_sends(sub - 1)
         if sub < heads:
@@ -496,8 +496,9 @@
             for d in order:
                 dkv_copy(i, h, d, me).start()
         if h == 0:
-            combine(SUBS - 1)
-            second_sends(SUBS - 1)
+            for sub in (SUBS - 2, SUBS - 1):
+                combine(sub)
+                second_sends(sub)
     dq_copy(b_last, me).start()
     dq_copy(t, me).start()
     own_dkv = [
@@ -614,13 +615,18 @@
         pltpu.make_async_copy(norm, norm_out, out_sem.at[2]),
         pltpu.make_async_copy(turned, w_out, out_sem.at[3]),
     ]
+    small_stores = list(stores)
+    for i, part, k in pieces[:2]:
+        loads[2 + k].wait()
+        stores.append(pltpu.make_async_copy(rows.at[i, part], outs[i].at[part], out_sem.at[4 + k]))
+        stores[-1].start()
     loads[0].wait()
     loads[1].wait()
     norm[...] = small[2:3, :]
     turned[...] = jnp.transpose(block[...])
-    for store in stores:
+    for store in small_stores:
         store.start()
-    for i, part, k in pieces:
+    for i, part, k in pieces[2:]:
         loads[2 + k].wait()
         stores.append(pltpu.make_async_copy(rows.at[i, part], outs[i].at[part], out_sem.at[4 + k]))
         stores[-1].start()

time: 245 us -> 245 us (level)
  no operation moved by 1% of the time
where the time goes in v6:
time: 245 us; the launch traced here: 244 us
  Pallas kernels  244 us (100%)
    pallas_call x1, Pallas kernels, local(): pl.pallas_call(functools.partial(kernel, n, side), out_shape=(struct((tok...  241 us

profile of v6, /device:TPU:1, one launch (start us, length us, event | category | flops | bytes accessed | tf_op | source)
XLA Modules:
  0.0 244.4 jit_solution(13061486675431177997)
XLA Ops:
  0.6 240.8 %fused.1 = (bf16[128,3072]{1,0:T(8,128)(2,1)}, bf16[128,3072]{1,0:T(8,128)(2,1)}, bf16[128,3072]{1,0:T(8,128)(2,1)}, f32[384,192]{1,0:T(8,128)}, f32[8,128]{1,0:T(8,128)}) custom-call(bf16[128,3072]{1,0:T(8,128)(2,1)} %bitcast.16, bf16[128,3072]{1,0:T(8,128)(2,1)} %bitcast.17, bf16[128,3072]{1,0:T(8,128)(2,1)} %bitcast.18, bf16[128,6144]{1,0:T(8,128)(2,1)} %bitcast.15, ...), custom_call_target="tpu_custom_call" | custom-call | tf_op jit(solution)/shard_map/fused/pallas_call | solution.py:648
  241.4 2.8 %write.1 = (bf16[128,3072]{1,0:T(8,128)(2,1)}, bf16[128,3072]{1,0:T(8,128)(2,1)}, bf16[128,3072]{1,0:T(8,128)(2,1)}, f32[192,384]{1,0:T(8,128)}, f32[1,128]{1,0:...) custom-call(bf16[128,3072]{1,0:T(8,128)(2,1)} %get-tuple-element.19.dq_in, bf16[128,3072]{1,0:T(8,128)(2,1)} %get-tuple-element.20.dk_in, ...), custom_call_target="tpu_custom_call" | custom-call | tf_op jit(solution)/shard_map/write/pallas_call | solution.py:730
